TPU v7x, 8 devices: a whole 2x2x1 slice. The times are simulated.
8 devices in a mesh: dp: 2 (over z, y), sp: 4 (over x, core).
Axes of the slice: x: 2, y: 2, z: 1, core: 2. Of those that a mesh axis runs over, the one named last changes fastest.
Arguments:
- signal: bfloat16 [65536, 768], P(('dp', 'sp')), parts along dimension 0
- w_first: bfloat16 [8, 256, 2, 128, 128], P(None, 'sp')
- w_second: bfloat16 [8, 256, 2, 128, 128], P(None, 'sp')
Outputs:
- output: bfloat16 [65536, 768], P(('dp', 'sp')), parts along dimension 0
There are 2 independent parts. A program takes and returns all parts, laid end to end along the dimension named above; an argument that names none is the same for every part.
All inputs are finite; a program needn't handle non-finite values.
Results may differ from a plain program's by a relative error of at most 0.02.
Values are sent between devices in bfloat16 or wider.
A program may use at most 1 GiB of HBM per device.

v0:
```python
import functools
import math

import jax
import jax.numpy as jnp
from jax import lax
from jax.experimental import pallas as pl
from jax.experimental.pallas import tpu as pltpu
from jax.sharding import PartitionSpec as P


WIDTH = 256
LAST_PIECES = (32, 16, 8, 4, 2, 2)
FIRST_PIECES = (4, 60)
TAIL_BLOCKS = 4

ERFC_P = (2.326819970068386e-2, -1.387039388740657e-1, 3.687424674597105e-1, -5.824733027278666e-1, 6.210004621745983e-1,
          -4.944515323274145e-1, 3.404879937665872e-1, -2.741127028184656e-1, 5.638259427386472e-1)
ERFC_R = (-1.047766399936249e1, 1.297719955372516e1, -7.495518717768503e0, 2.921019019210786e0, -1.015265279202700e0,
          4.218463358204948e-1, -2.820767439740514e-1, 5.641895067754075e-1)


def horner(coeffs, y):
    total = jnp.full_like(y, coeffs[0])
    for c in coeffs[1:]:
        total = total * y + c
    return total


def gelu(x):
    a = x * (-(0.5 ** 0.5))
    mag = jnp.abs(a)
    far = jnp.maximum(mag, 1.0)
    q = 1.0 / far
    y = q * q
    poly = jnp.where(far < 2.0, horner(ERFC_P, y), horner(ERFC_R, y))
    tail = jnp.exp(-far * far) * q * poly
    tail = jnp.where(a < 0.0, 2.0 - tail, tail)
    return 0.5 * x * jnp.where(mag < 1.0, 1.0 - lax.erf(a), tail)


def mix(w_own, w_cross, z_own, z_cross):
    weights = jnp.concatenate([w_own, w_cross], axis=1)
    blocks = jnp.concatenate([z_own, z_cross], axis=0)
    return jnp.dot(weights, blocks, preferred_element_type=jnp.float32)


def cross_kernel(blocks, *refs):
    own, partner, w, out = refs[0], refs[1], refs[2], refs[-1]
    size = w.shape[-1]
    for b in range(blocks):
        rows = pl.ds(b * size, size)
        out[rows, :] = mix(w[0, b, 0], w[0, b, 1], own[rows, :], partner[rows, :]).astype(out.dtype)


def cross_stage(own, partner, weights, stage, first, count, width, own_at, partner_at, out_shape, out_at, into=None, after=()):
    size, blocks = weights.shape[-1], math.gcd(first, count, 8)
    any_space = pl.BlockSpec(memory_space=pl.ANY)

    def spec(at):
        row, col = at
        return pl.BlockSpec((blocks * size, width), lambda g: (row // blocks + g, col))

    operands = [own, partner, weights]
    in_specs = [
        spec(own_at),
        spec(partner_at),
        pl.BlockSpec((1, blocks, 2, size, size), lambda g: (stage, first // blocks + g, 0, 0, 0)),
    ]
    aliases = {}
    if into is not None:
        aliases = {len(operands): 0}
        operands.append(into)
    operands += after
    in_specs += [any_space] * (len(operands) - len(in_specs))
    rows = count * size
    return pl.pallas_call(
        functools.partial(cross_kernel, blocks),
        grid=(count // blocks,),
        out_shape=jax.ShapeDtypeStruct(out_shape, own.dtype),
        in_specs=in_specs,
        out_specs=spec(out_at),
        input_output_aliases=aliases,
        compiler_params=pltpu.CompilerParams(dimension_semantics=("arbitrary",)),
        cost_estimate=pl.CostEstimate(
            flops=4 * rows * size * width, bytes_accessed=6 * rows * width + 4 * rows * size, transcendentals=0),
        name="cross_stage",
    )(*operands)


def tail_kernel(count, first, col, own, partner, w, into, out, mixed, sem):
    del into
    size, width = w.shape[-1], own.shape[1]
    copies = []
    for b in range(count):
        rows = pl.ds(b * size, size)
        mixed[rows, :] = mix(w[b, 0], w[b, 1], own[rows, :], partner[rows, :]).astype(mixed.dtype)
        target = out.at[pl.ds((first + b) * size, size), pl.ds(col * width, width)]
        copies.append(pltpu.make_async_copy(mixed.at[rows, :], target, sem.at[b]))
        copies[-1].start()
    for copy in copies:
        copy.wait()


def tail_stage(own, partner, weights, first, count, col, into):
    size, width = weights.shape[-1], own.shape[1]
    vmem, any_space = pl.BlockSpec(memory_space=pltpu.VMEM), pl.BlockSpec(memory_space=pl.ANY)
    return pl.pallas_call(
        functools.partial(tail_kernel, count, first, col),
        out_shape=jax.ShapeDtypeStruct(into.shape, into.dtype),
        in_specs=[vmem, vmem, vmem, any_space],
        out_specs=any_space,
        scratch_shapes=[pltpu.VMEM((count * size, width), own.dtype), pltpu.SemaphoreType.DMA((count,))],
        input_output_aliases={3: 0},
        compiler_params=pltpu.CompilerParams(vmem_limit_bytes=4 * 1024 * 1024),
        cost_estimate=pl.CostEstimate(
            flops=4 * count * size * size * width, bytes_accessed=2 * count * size * width, transcendentals=0),
        name="tail_stage",
    )(own, partner, weights, into)


def local_kernel(first_steps, own, partner, wf, ws, out, other):
    step = pl.program_id(0)
    local, size = wf.shape[1], wf.shape[-1]

    @pl.when(step == 0)
    def _():
        def body(b, carry):
            rows = pl.ds(pl.multiple_of(b * size, size), size)
            out[rows, :] = mix(wf[0, b, 0], wf[0, b, 1], own[rows, :], partner[rows, :]).astype(out.dtype)
            return carry

        lax.fori_loop(0, local, body, 0, unroll=8)

    def stage(w, src, dst, shift, act):
        def body(p, carry):
            i = lax.shift_left(lax.shift_right_logical(p, shift), shift + 1) + (p & (lax.shift_left(1, shift) - 1))
            j = i + lax.shift_left(1, shift)
            ri = pl.ds(pl.multiple_of(i * size, size), size)
            rj = pl.ds(pl.multiple_of(j * size, size), size)
            zi, zj = src[ri, :], src[rj, :]
            blocks = jnp.concatenate([zi, zj], axis=0)
            weights = jnp.concatenate([
                jnp.concatenate([w[0, i, 0], w[0, i, 1]], axis=1),
                jnp.concatenate([w[0, j, 1], w[0, j, 0]], axis=1),
            ], axis=0)
            mixed = jnp.dot(weights, blocks, preferred_element_type=jnp.float32)
            mixed = mixed.astype(dst.dtype)
            if act:
                mixed = gelu(mixed.astype(jnp.float32)).astype(dst.dtype)
            dst[ri, :] = mixed[:size]
            dst[rj, :] = mixed[size:]
            return carry

        lax.fori_loop(0, local // 2, body, 0, unroll=1 if act else 4)

    odd = (step % 2) == 1

    @pl.when(jnp.logical_and(jnp.logical_and(step >= 1, step < first_steps), odd))
    def _():
        stage(wf, out, other, first_steps - step, False)

    @pl.when(jnp.logical_and(jnp.logical_and(step >= 1, step < first_steps), jnp.logical_not(odd)))
    def _():
        stage(wf, other, out, first_steps - step, False)

    @pl.when(step == first_steps)
    def _():
        if first_steps % 2:
            stage(wf, out, other, 0, True)
        else:
            stage(wf, other, out, 0, True)

    @pl.when(jnp.logical_and(step > first_steps, odd))
    def _():
        stage(ws, out, other, step - first_steps - 1, False)

    @pl.when(jnp.logical_and(step > first_steps, jnp.logical_not(odd)))
    def _():
        stage(ws, other, out, step - first_steps - 1, False)


def local_stages(own, partner, w_first, w_second, skip):
    stages, local, _, size, _ = w_first.shape
    rows, width = own.shape
    first_steps = stages - skip
    steps = 1 + 2 * first_steps
    whole = pl.BlockSpec((rows, width), lambda t: (0, 0))
    w_block = (1, local, 2, size, size)
    flops = 4 * rows * size * width * steps
    return pl.pallas_call(
        functools.partial(local_kernel, first_steps),
        grid=(steps,),
        out_shape=jax.ShapeDtypeStruct((rows, width), own.dtype),
        in_specs=[
            whole,
            whole,
            pl.BlockSpec(w_block, lambda t: (jnp.minimum(t + skip - 1, stages - 1), 0, 0, 0, 0)),
            pl.BlockSpec(w_block, lambda t: (jnp.maximum(t - first_steps - 1, 0), 0, 0, 0, 0)),
        ],
        out_specs=whole,
        scratch_shapes=[pltpu.VMEM((rows, width), own.dtype)],
        compiler_params=pltpu.CompilerParams(dimension_semantics=("arbitrary",), vmem_limit_bytes=60 * 1024 * 1024),
        cost_estimate=pl.CostEstimate(flops=flops, bytes_accessed=6 * rows * width + 4 * rows * size * steps, transcendentals=0),
        name="local_stages",
    )(own, partner, w_first, w_second)


def solution(mesh):
    groups = mesh.shape["sp"]

    def swap(array, dev_step):
        return lax.ppermute(array, "sp", [(device, device ^ dev_step) for device in range(groups)])

    def device_program(signal, w_first, w_second):
        stages, local = w_first.shape[:2]
        rows, cols = signal.shape
        size = w_first.shape[-1]
        far = (2 ** (stages - 1)) // local
        near = far // 2
        width = WIDTH
        sent, source = [], signal
        for c in range(cols // width):
            pieces = FIRST_PIECES if c == 0 else (local,)
            first, parts = 0, []
            for count in pieces:
                piece = source[first * size:(first + count) * size, c * width:(c + 1) * width]
                source, piece = lax.optimization_barrier((source, piece))
                parts.append((first, count, swap(piece, far)))
                first += count
            sent.append(parts)
        late, done = [], ()
        for c, parts in enumerate(sent):
            act = None
            for first, count, partner in parts:
                act = cross_stage(signal, partner, w_first, 0, first, count, width, (first, c), (0, 0), (rows, width), (first, 0),
                                  into=act, after=done)
            act = local_stages(act, swap(act, near), w_first, w_second, 2)
            partner = swap(act, near)
            pieces = LAST_PIECES if c == cols // width - 1 else (local,)
            first = 0
            for count in pieces:
                piece = cross_stage(act, partner, w_second, stages - 2, first, count, width, (first, 0), (first, 0),
                                    (count * size, width), (0, 0))
                late.append((c, first, count, piece, swap(piece, far)))
                first += count
            done = [piece]
        result = None
        for c, first, count, piece, partner in late:
            if count <= TAIL_BLOCKS:
                result = tail_stage(piece, partner, w_second[stages - 1, first:first + count], first, count, c, result)
                continue
            result = cross_stage(piece, partner, w_second, stages - 1, first, count, width, (0, 0), (0, 0), (rows, cols), (first, c),
                                 into=result, after=done)
        return result

    row_spec = P(("dp", "sp"), None)
    weight_spec = P(None, "sp", None, None, None)
    return jax.shard_map(device_program, mesh=mesh, in_specs=(row_spec, weight_spec, weight_spec), out_specs=row_spec, check_vma=False)
```

profile of v0, /device:TPU:0, one launch (start us, length us, event | category | flops | bytes accessed | tf_op | source)
XLA Modules:
  0.0 801.2 jit_solution(4448114253528217434)
XLA Ops:
  1.0 4.2 slice.22
  5.2 3.3 collective-permute-start.2
  8.5 90.8 %collective-permute-done.3.refs_1_ = bf16[512,256]{1,0:T(8,128)(2,1)S(1)} collective-permute-done((bf16[512,256]{1,0:T(8,128)(2,1)S(1)}, bf16[512,256]{1,0:T(8,128)(2,1)S(1)}, u32[]{:S(2)}, u32[]{:S(2)}) %collective-permute-start.3) | collective-permute-done | bytes 262176 | tf_op jit(solution)/shard_map/ppermute | solution.py:213
  102.1 12.7 %cross_stage.18.own = bf16[8192,256]{1,0:T(8,128)(2,1)} custom-call(bf16[8192,768]{1,0:T(8,128)(2,1)} %refs_0_.7, bf16[7680,256]{1,0:T(8,128)(2,1)} %collective-permute-done.2.refs_1_, bf16[8,64,2,128,128]{4,3,2,1,0:T(8,128)(2,1)} %wf.5, bf16[8192,256]{1,0:T(8,128)(2,1)} %cross_stage.17.refs_3_), custom_call_target="tpu_custom_call", output_to_operand_aliasing={{}: (3, {})} | custom-call | flops 1006632960 | bytes 15728640 | tf_op jit(solution)/shard_map/cross_stage/pallas_call | solution.py:77
  114.8 7.5 collective-permute-done.4.partner
  122.3 58.3 %local_stages.3.refs_0_ = bf16[8192,256]{1,0:T(8,128)(2,1)} custom-call(bf16[8192,256]{1,0:T(8,128)(2,1)} %cross_stage.18.own, bf16[8192,256]{1,0:T(8,128)(2,1)} %collective-permute-done.4.partner, bf16[8,64,2,128,128]{4,3,2,1,0:T(8,128)(2,1)} %wf.5, bf16[8,64,2,128,128]{4,3,2,1,0:T(8,128)(2,1)} %refs_2_.33), custom_call_target="tpu_custom_call" | custom-call | flops 13958643712 | bytes 67108864 | tf_op jit(solution)/shard_map/local_stages/pallas_call | solution.py:191
  180.7 4.5 slice.23
  188.1 9.3 %cross_stage.19.refs_3_.refs_0_ = bf16[8192,256]{1,0:T(8,128)(2,1)} custom-call(bf16[8192,256]{1,0:T(8,128)(2,1)} %local_stages.3.refs_0_, bf16[8192,256]{1,0:T(8,128)(2,1)} %collective-permute-done.5.refs_1_, bf16[8,64,2,128,128]{4,3,2,1,0:T(8,128)(2,1)} %refs_2_.33), custom_call_target="tpu_custom_call" | custom-call | flops 1073741824 | bytes 16777216 | tf_op jit(solution)/shard_map/cross_stage/pallas_call | solution.py:77
  197.4 81.0 %collective-permute-done.1.refs_1_ = bf16[8192,256]{1,0:T(8,128)(2,1)} collective-permute-done((bf16[8192,256]{1,0:T(8,128)(2,1)}, bf16[8192,256]{1,0:T(8,128)(2,1)}, u32[]{:S(2)}, u32[]{:S(2)}) %collective-permute-start.1) | collective-permute-done | bytes 4194336 | tf_op jit(solution)/shard_map/ppermute | solution.py:213
  278.4 9.3 %cross_stage.20.own = bf16[8192,256]{1,0:T(8,128)(2,1)} custom-call(bf16[8192,768]{1,0:T(8,128)(2,1)} %refs_0_.7, bf16[8192,256]{1,0:T(8,128)(2,1)} %collective-permute-done.1.refs_1_, bf16[8,64,2,128,128]{4,3,2,1,0:T(8,128)(2,1)} %wf.5, bf16[8192,256]{1,0:T(8,128)(2,1)} %cross_stage.19.refs_3_.refs_0_), custom_call_target="tpu_custom_call" | custom-call | flops 1073741824 | bytes 16777216 | tf_op jit(solution)/shard_map/cross_stage/pallas_call | solution.py:77
  287.7 7.5 collective-permute-done.6.partner
  295.2 58.3 %local_stages.4.refs_0_ = bf16[8192,256]{1,0:T(8,128)(2,1)} custom-call(bf16[8192,256]{1,0:T(8,128)(2,1)} %cross_stage.20.own, bf16[8192,256]{1,0:T(8,128)(2,1)} %collective-permute-done.6.partner, bf16[8,64,2,128,128]{4,3,2,1,0:T(8,128)(2,1)} %wf.5, bf16[8,64,2,128,128]{4,3,2,1,0:T(8,128)(2,1)} %refs_2_.33), custom_call_target="tpu_custom_call" | custom-call | flops 13958643712 | bytes 67108864 | tf_op jit(solution)/shard_map/local_stages/pallas_call | solution.py:191
  353.7 4.5 slice.24
  361.0 9.3 %cross_stage.21.refs_3_.refs_0_ = bf16[8192,256]{1,0:T(8,128)(2,1)} custom-call(bf16[8192,256]{1,0:T(8,128)(2,1)} %local_stages.4.refs_0_, bf16[8192,256]{1,0:T(8,128)(2,1)} %collective-permute-done.7.refs_1_, bf16[8,64,2,128,128]{4,3,2,1,0:T(8,128)(2,1)} %refs_2_.33), custom_call_target="tpu_custom_call" | custom-call | flops 1073741824 | bytes 16777216 | tf_op jit(solution)/shard_map/cross_stage/pallas_call | solution.py:77
  370.4 81.0 %collective-permute-done.refs_1_ = bf16[8192,256]{1,0:T(8,128)(2,1)} collective-permute-done((bf16[8192,256]{1,0:T(8,128)(2,1)}, bf16[8192,256]{1,0:T(8,128)(2,1)}, u32[]{:S(2)}, u32[]{:S(2)}) %collective-permute-start) | collective-permute-done | bytes 4194336 | tf_op jit(solution)/shard_map/ppermute | solution.py:213
  451.3 9.3 %cross_stage.22.own = bf16[8192,256]{1,0:T(8,128)(2,1)} custom-call(bf16[8192,768]{1,0:T(8,128)(2,1)} %refs_0_.7, bf16[8192,256]{1,0:T(8,128)(2,1)} %collective-permute-done.refs_1_, bf16[8,64,2,128,128]{4,3,2,1,0:T(8,128)(2,1)} %wf.5, bf16[8192,256]{1,0:T(8,128)(2,1)} %cross_stage.21.refs_3_.refs_0_), custom_call_target="tpu_custom_call" | custom-call | flops 1073741824 | bytes 16777216 | tf_op jit(solution)/shard_map/cross_stage/pallas_call | solution.py:77
  460.6 7.5 collective-permute-done.8.partner
  468.1 58.3 %local_stages.5.refs_0_ = bf16[8192,256]{1,0:T(8,128)(2,1)} custom-call(bf16[8192,256]{1,0:T(8,128)(2,1)} %cross_stage.22.own, bf16[8192,256]{1,0:T(8,128)(2,1)} %collective-permute-done.8.partner, bf16[8,64,2,128,128]{4,3,2,1,0:T(8,128)(2,1)} %wf.5, bf16[8,64,2,128,128]{4,3,2,1,0:T(8,128)(2,1)} %refs_2_.33), custom_call_target="tpu_custom_call" | custom-call | flops 13958643712 | bytes 67108864 | tf_op jit(solution)/shard_map/local_stages/pallas_call | solution.py:191
  528.6 5.3 collective-permute-done.9.refs_1_
  533.9 5.1 cross_stage.28.refs_0_
  540.8 2.9 cross_stage.27.refs_0_
  556.1 64.3 %collective-permute-done.17.refs_1_ = bf16[8192,256]{1,0:T(8,128)(2,1)} collective-permute-done((bf16[8192,256]{1,0:T(8,128)(2,1)}, bf16[8192,256]{1,0:T(8,128)(2,1)}, u32[]{:S(2)}, u32[]{:S(2)}) %collective-permute-start.17) | collective-permute-done | bytes 4194336 | tf_op jit(solution)/shard_map/ppermute | solution.py:213
  622.1 9.3 %cross_stage.29.refs_3_ = bf16[8192,768]{1,0:T(8,128)(2,1)} custom-call(bf16[8192,256]{1,0:T(8,128)(2,1)} %cross_stage.19.refs_3_.refs_0_, bf16[8192,256]{1,0:T(8,128)(2,1)} %collective-permute-done.17.refs_1_, bf16[8,64,2,128,128]{4,3,2,1,0:T(8,128)(2,1)} %refs_2_.33, bf16[256,256]{1,0:T(8,128)(2,1)} %cross_stage.23.refs_3_.refs_4_.own), custom_call_target="tpu_custom_call" | custom-call | flops 1073741824 | bytes 16777216 | tf_op jit(solution)/shard_map/cross_stage/pallas_call | solution.py:77
  631.4 78.8 %collective-permute-done.16.refs_1_ = bf16[8192,256]{1,0:T(8,128)(2,1)} collective-permute-done((bf16[8192,256]{1,0:T(8,128)(2,1)}, bf16[8192,256]{1,0:T(8,128)(2,1)}, u32[]{:S(2)}, u32[]{:S(2)}) %collective-permute-start.16) | collective-permute-done | bytes 4194336 | tf_op jit(solution)/shard_map/ppermute | solution.py:213
  712.0 43.1 %collective-permute-done.15.refs_1_ = bf16[4096,256]{1,0:T(8,128)(2,1)S(1)} collective-permute-done((bf16[4096,256]{1,0:T(8,128)(2,1)}, bf16[4096,256]{1,0:T(8,128)(2,1)S(1)}, u32[]{:S(2)}, u32[]{:S(2)}) %collective-permute-start.15) | collective-permute-done | bytes 2097184 | tf_op jit(solution)/shard_map/ppermute | solution.py:213
  756.8 9.3 %cross_stage.30.refs_3_ = bf16[8192,768]{1,0:T(8,128)(2,1)} custom-call(bf16[8192,256]{1,0:T(8,128)(2,1)} %cross_stage.21.refs_3_.refs_0_, bf16[8192,256]{1,0:T(8,128)(2,1)} %collective-permute-done.16.refs_1_, bf16[8,64,2,128,128]{4,3,2,1,0:T(8,128)(2,1)} %refs_2_.33, bf16[8192,768]{1,0:T(8,128)(2,1)} %cross_stage.29.refs_3_, ...), custom_call_target="tpu_custom_call", output_to_operand_aliasing={{}: (3, {})} | custom-call | flops 1073741824 | bytes 16777216 | tf_op jit(solution)/shard_map/cross_stage/pallas_call | solution.py:77
  766.1 5.1 cross_stage.31.refs_3_
  771.2 6.4 collective-permute-done.14.refs_1_
  777.6 2.9 cross_stage.32.refs_3_
  780.5 8.3 %collective-permute-done.13.refs_1_ = bf16[1024,256]{1,0:T(8,128)(2,1)} collective-permute-done((bf16[1024,256]{1,0:T(8,128)(2,1)}, bf16[1024,256]{1,0:T(8,128)(2,1)}, u32[]{:S(2)}, u32[]{:S(2)}) %collective-permute-start.13) | collective-permute-done | bytes 524320 | tf_op jit(solution)/shard_map/ppermute | solution.py:213
  791.3 3.1 collective-permute-done.12.partner
  795.3 4.1 collective-permute-done.11.partner
  (45 shorter events, 36.5 us)
Async XLA Ops:
  5.2 96.9 %collective-permute-start.2 = (bf16[7680,256]{1,0:T(8,128)(2,1)}, bf16[7680,256]{1,0:T(8,128)(2,1)}, u32[]{:S(2)}, u32[]{:S(2)}) collective-permute-start(bf16[7680,256]{1,0:T(8,128)(2,1)} %slice.22), channel_id=1, source_target_pairs={{0,2},{1,3},{2,0},{3,1},{4,6},{5,7},{6,4},{7,5}} | collective-permute-start | bytes 11796488 | tf_op jit(solution)/shard_map/ppermute | solution.py:213
  8.5 90.8 %collective-permute-start.3 = (bf16[512,256]{1,0:T(8,128)(2,1)S(1)}, bf16[512,256]{1,0:T(8,128)(2,1)S(1)}, u32[]{:S(2)}, u32[]{:S(2)}) collective-permute-start(bf16[512,256]{1,0:T(8,128)(2,1)S(1)} %slice.21), channel_id=1, source_target_pairs={{0,2},{1,3},{2,0},{3,1},{4,6},{5,7},{6,4},{7,5}} | collective-permute-start | bytes 786440 | tf_op jit(solution)/shard_map/ppermute | solution.py:213
  99.3 0.8 copy-start.5
  114.8 7.5 collective-permute-start.4
  180.6 7.5 collective-permute-start.5
  185.2 93.2 %collective-permute-start.1 = (bf16[8192,256]{1,0:T(8,128)(2,1)}, bf16[8192,256]{1,0:T(8,128)(2,1)}, u32[]{:S(2)}, u32[]{:S(2)}) collective-permute-start(bf16[8192,256]{1,0:T(8,128)(2,1)} %slice.23), channel_id=1, source_target_pairs={{0,2},{1,3},{2,0},{3,1},{4,6},{5,7},{6,4},{7,5}} | collective-permute-start | bytes 12582920 | tf_op jit(solution)/shard_map/ppermute | solution.py:213
  287.7 7.5 collective-permute-start.6
  353.5 7.5 collective-permute-start.7
  358.1 93.2 %collective-permute-start = (bf16[8192,256]{1,0:T(8,128)(2,1)}, bf16[8192,256]{1,0:T(8,128)(2,1)}, u32[]{:S(2)}, u32[]{:S(2)}) collective-permute-start(bf16[8192,256]{1,0:T(8,128)(2,1)} %slice.24), channel_id=1, source_target_pairs={{0,2},{1,3},{2,0},{3,1},{4,6},{5,7},{6,4},{7,5}} | collective-permute-start | bytes 12582920 | tf_op jit(solution)/shard_map/ppermute | solution.py:213
  460.6 7.5 collective-permute-start.8
  526.4 7.5 collective-permute-start.9
  526.6 93.8 %collective-permute-start.17 = (bf16[8192,256]{1,0:T(8,128)(2,1)}, bf16[8192,256]{1,0:T(8,128)(2,1)}, u32[]{:S(2)}, u32[]{:S(2)}) collective-permute-start(bf16[8192,256]{1,0:T(8,128)(2,1)} %cross_stage.19.refs_3_.refs_0_), channel_id=1, source_target_pairs={{0,2},{1,3},{2,0},{3,1},{4,6},{5,7},{6,4},{7,5}} | collective-permute-start | bytes 12582920 | tf_op jit(solution)/shard_map/ppermute | solution.py:213
  528.3 181.9 %collective-permute-start.16 = (bf16[8192,256]{1,0:T(8,128)(2,1)}, bf16[8192,256]{1,0:T(8,128)(2,1)}, u32[]{:S(2)}, u32[]{:S(2)}) collective-permute-start(bf16[8192,256]{1,0:T(8,128)(2,1)} %cross_stage.21.refs_3_.refs_0_), channel_id=1, source_target_pairs={{0,2},{1,3},{2,0},{3,1},{4,6},{5,7},{6,4},{7,5}} | collective-permute-start | bytes 12582920 | tf_op jit(solution)/shard_map/ppermute | solution.py:213
  539.1 216.0 %collective-permute-start.15 = (bf16[4096,256]{1,0:T(8,128)(2,1)}, bf16[4096,256]{1,0:T(8,128)(2,1)S(1)}, u32[]{:S(2)}, u32[]{:S(2)}) collective-permute-start(bf16[4096,256]{1,0:T(8,128)(2,1)} %cross_stage.28.refs_0_), channel_id=1, source_target_pairs={{0,2},{1,3},{2,0},{3,1},{4,6},{5,7},{6,4},{7,5}} | collective-permute-start | bytes 6291464 | tf_op jit(solution)/shard_map/ppermute | solution.py:213
  543.8 233.9 %collective-permute-start.14 = (bf16[2048,256]{1,0:T(8,128)(2,1)}, bf16[2048,256]{1,0:T(8,128)(2,1)}, u32[]{:S(2)}, u32[]{:S(2)}) collective-permute-start(bf16[2048,256]{1,0:T(8,128)(2,1)} %cross_stage.27.refs_0_), channel_id=1, source_target_pairs={{0,2},{1,3},{2,0},{3,1},{4,6},{5,7},{6,4},{7,5}} | collective-permute-start | bytes 3145736 | tf_op jit(solution)/shard_map/ppermute | solution.py:213
  546.5 242.3 %collective-permute-start.13 = (bf16[1024,256]{1,0:T(8,128)(2,1)}, bf16[1024,256]{1,0:T(8,128)(2,1)}, u32[]{:S(2)}, u32[]{:S(2)}) collective-permute-start(bf16[1024,256]{1,0:T(8,128)(2,1)} %cross_stage.26.refs_0_), channel_id=1, source_target_pairs={{0,2},{1,3},{2,0},{3,1},{4,6},{5,7},{6,4},{7,5}} | collective-permute-start | bytes 1572872 | tf_op jit(solution)/shard_map/ppermute | solution.py:213
  556.1 154.1 %copy-start = (bf16[256,256]{1,0:T(8,128)(2,1)S(1)}, bf16[256,256]{1,0:T(8,128)(2,1)}, u32[]{:S(2)}) copy-start(bf16[256,256]{1,0:T(8,128)(2,1)} %cross_stage.23.refs_3_.refs_4_.own) | copy-start | bytes 393220
  556.1 199.0 %copy-start.3 = (bf16[256,256]{1,0:T(8,128)(2,1)S(1)}, bf16[256,256]{1,0:T(8,128)(2,1)}, u32[]{:S(2)}) copy-start(bf16[256,256]{1,0:T(8,128)(2,1)} %cross_stage.24.own) | copy-start | bytes 393220
  620.3 174.0 %collective-permute-start.12 = (bf16[512,256]{1,0:T(8,128)(2,1)}, bf16[512,256]{1,0:T(8,128)(2,1)S(1)}, u32[]{:S(2)}, u32[]{:S(2)}) collective-permute-start(bf16[512,256]{1,0:T(8,128)(2,1)} %cross_stage.25.own), channel_id=1, source_target_pairs={{0,2},{1,3},{2,0},{3,1},{4,6},{5,7},{6,4},{7,5}} | collective-permute-start | bytes 786440 | tf_op jit(solution)/shard_map/ppermute | solution.py:213
  710.2 90.1 %collective-permute-start.10 = (bf16[256,256]{1,0:T(8,128)(2,1)S(1)}, bf16[256,256]{1,0:T(8,128)(2,1)S(1)}, u32[]{:S(2)}, u32[]{:S(2)}) collective-permute-start(bf16[256,256]{1,0:T(8,128)(2,1)S(1)} %copy-done), channel_id=1, source_target_pairs={{0,2},{1,3},{2,0},{3,1},{4,6},{5,7},{6,4},{7,5}} | collective-permute-start | bytes 393224 | tf_op jit(solution)/shard_map/ppermute | solution.py:213
  755.0 11.0 %copy-start.4 = (bf16[4096,256]{1,0:T(8,128)(2,1)}, bf16[4096,256]{1,0:T(8,128)(2,1)S(1)}, u32[]{:S(2)}) copy-start(bf16[4096,256]{1,0:T(8,128)(2,1)S(1)} %collective-permute-done.15.refs_1_) | copy-start | bytes 6291460
  755.0 44.4 %collective-permute-start.11 = (bf16[256,256]{1,0:T(8,128)(2,1)S(1)}, bf16[256,256]{1,0:T(8,128)(2,1)S(1)}, u32[]{:S(2)}, u32[]{:S(2)}) collective-permute-start(bf16[256,256]{1,0:T(8,128)(2,1)S(1)} %copy-done.3), channel_id=1, source_target_pairs={{0,2},{1,3},{2,0},{3,1},{4,6},{5,7},{6,4},{7,5}} | collective-permute-start | bytes 393224 | tf_op jit(solution)/shard_map/ppermute | solution.py:213
  780.5 13.8 %copy-start.2 = (bf16[512,256]{1,0:T(8,128)(2,1)S(1)}, bf16[512,256]{1,0:T(8,128)(2,1)}, u32[]{:S(2)}) copy-start(bf16[512,256]{1,0:T(8,128)(2,1)} %cross_stage.25.own) | copy-start | bytes 786436
  799.4 0.9 copy-start.1
where the time goes:
time: 803 us; the launch traced here: 801 us
  waiting for transfers between devices  491 us (61%)
  Pallas kernels  275 us (34%)
  starting transfers between devices  18.3 us (2%)
  local copies, waits for them, and re-layouts  16.9 us (2%)
    ppermute x18, waiting for transfers between devices, swap(): lax.ppermute(array, 'sp', [(device, device ^ dev_step) for device in rang...  491 us
    pallas_call x3, Pallas kernels, local_stages(): pl.pallas_call(functools.partial(local_kernel, first_steps), grid=(steps,...  175 us
    pallas_call x17, Pallas kernels, cross_stage(): pl.pallas_call(functools.partial(cross_kernel, blocks), grid=(count // bl...  97.4 us
    ppermute x18, starting transfers between devices, swap(): lax.ppermute(array, 'sp', [(device, device ^ dev_step) for device in rang...  18.3 us
  transfers between devices with their start and end apart: 18, of which 16 were waited for; matrix products, arithmetic and copies ran while one was open for 1% of the time, Pallas kernels for 8%

commit v1 on v0

--- a/solution.py
+++ b/solution.py
@@ -10,9 +10,9 @@
 
 
 WIDTH = 256
-LAST_PIECES = (32, 16, 8, 4, 2, 2)
-FIRST_PIECES = (4, 60)
-TAIL_BLOCKS = 4
+LAST_PIECES = (52, 8, 4)
+FIRST_PIECES = (8, 56)
+TAIL_BLOCKS = 8
 
 ERFC_P = (2.326819970068386e-2, -1.387039388740657e-1, 3.687424674597105e-1, -5.824733027278666e-1, 6.210004621745983e-1,
           -4.944515323274145e-1, 3.404879937665872e-1, -2.741127028184656e-1, 5.638259427386472e-1)

time: 803 us -> 799 us (level)
    ppermute x18 -> x15, starting transfers between devices: 18.3 us -> 13 us  [swap(): lax.ppermute(array, 'sp', [(device, device ^ dev_step) for device in rang...]
    ppermute x18 -> x15, waiting for transfers between devices: 491 us -> 496 us  [swap(): lax.ppermute(array, 'sp', [(device, device ^ dev_step) for device in rang...]
    pallas_call x17 -> x12, Pallas kernels: 97.4 us -> 93.8 us  [cross_stage(): pl.pallas_call(functools.partial(cross_kernel, blocks), grid=(count // bl...]
  transfers between devices with their start and end apart: 18 -> 15, of which waited for: 16 -> 13; matrix products, arithmetic and copies ran while one was open for 1% -> 1% of each run, Pallas kernels for 8% -> 8%
where the time goes in v1:
time: 799 us; the launch traced here: 797 us
  waiting for transfers between devices  496 us (62%)
  Pallas kernels  271 us (34%)
  local copies, waits for them, and re-layouts  16.9 us (2%)
  starting transfers between devices  13 us (2%)
    ppermute x15, waiting for transfers between devices, swap(): lax.ppermute(array, 'sp', [(device, device ^ dev_step) for device in rang...  496 us
    pallas_call x3, Pallas kernels, local_stages(): pl.pallas_call(functools.partial(local_kernel, first_steps), grid=(steps,...  175 us
    pallas_call x12, Pallas kernels, cross_stage(): pl.pallas_call(functools.partial(cross_kernel, blocks), grid=(count // bl...  93.8 us
  transfers between devices with their start and end apart: 15, of which 13 were waited for; matrix products, arithmetic and copies ran while one was open for 1% of the time, Pallas kernels for 8%

profile of v1, /device:TPU:0, one launch (start us, length us, event | category | flops | bytes accessed | tf_op | source)
XLA Modules:
  0.0 796.9 jit_solution(1596039529354123198)
XLA Ops:
  1.1 4.1 slice.19
  5.1 3.3 collective-permute-start.2
  8.5 90.8 %collective-permute-done.3.refs_1_ = bf16[1024,256]{1,0:T(8,128)(2,1)S(1)} collective-permute-done((bf16[1024,256]{1,0:T(8,128)(2,1)S(1)}, bf16[1024,256]{1,0:T(8,128)(2,1)S(1)}, u32[]{:S(2)}, u32[]{:S(2)}) %collective-permute-start.3) | collective-permute-done | bytes 524320 | tf_op jit(solution)/shard_map/ppermute | solution.py:213
  100.0 2.5 cross_stage.12.refs_3_
  102.5 8.8 %cross_stage.13.own = bf16[8192,256]{1,0:T(8,128)(2,1)} custom-call(bf16[8192,768]{1,0:T(8,128)(2,1)} %refs_0_.7, bf16[7168,256]{1,0:T(8,128)(2,1)} %collective-permute-done.2.refs_1_, bf16[8,64,2,128,128]{4,3,2,1,0:T(8,128)(2,1)} %wf.5, bf16[8192,256]{1,0:T(8,128)(2,1)} %cross_stage.12.refs_3_), custom_call_target="tpu_custom_call", output_to_operand_aliasing={{}: (3, {})} | custom-call | flops 939524096 | bytes 14680064 | tf_op jit(solution)/shard_map/cross_stage/pallas_call | solution.py:77
  111.3 7.5 collective-permute-done.4.partner
  118.8 58.4 %local_stages.3.refs_0_ = bf16[8192,256]{1,0:T(8,128)(2,1)} custom-call(bf16[8192,256]{1,0:T(8,128)(2,1)} %cross_stage.13.own, bf16[8192,256]{1,0:T(8,128)(2,1)} %collective-permute-done.4.partner, bf16[8,64,2,128,128]{4,3,2,1,0:T(8,128)(2,1)} %wf.5, bf16[8,64,2,128,128]{4,3,2,1,0:T(8,128)(2,1)} %refs_2_.23), custom_call_target="tpu_custom_call" | custom-call | flops 13958643712 | bytes 67108864 | tf_op jit(solution)/shard_map/local_stages/pallas_call | solution.py:191
  177.3 4.5 slice.20
  181.8 1.7 collective-permute-start.1
  184.7 9.3 %cross_stage.14.refs_3_.refs_0_ = bf16[8192,256]{1,0:T(8,128)(2,1)} custom-call(bf16[8192,256]{1,0:T(8,128)(2,1)} %local_stages.3.refs_0_, bf16[8192,256]{1,0:T(8,128)(2,1)} %collective-permute-done.5.refs_1_, bf16[8,64,2,128,128]{4,3,2,1,0:T(8,128)(2,1)} %refs_2_.23), custom_call_target="tpu_custom_call" | custom-call | flops 1073741824 | bytes 16777216 | tf_op jit(solution)/shard_map/cross_stage/pallas_call | solution.py:77
  194.0 81.0 %collective-permute-done.1.refs_1_ = bf16[8192,256]{1,0:T(8,128)(2,1)} collective-permute-done((bf16[8192,256]{1,0:T(8,128)(2,1)}, bf16[8192,256]{1,0:T(8,128)(2,1)}, u32[]{:S(2)}, u32[]{:S(2)}) %collective-permute-start.1) | collective-permute-done | bytes 4194336 | tf_op jit(solution)/shard_map/ppermute | solution.py:213
  275.0 9.3 %cross_stage.15.own = bf16[8192,256]{1,0:T(8,128)(2,1)} custom-call(bf16[8192,768]{1,0:T(8,128)(2,1)} %refs_0_.7, bf16[8192,256]{1,0:T(8,128)(2,1)} %collective-permute-done.1.refs_1_, bf16[8,64,2,128,128]{4,3,2,1,0:T(8,128)(2,1)} %wf.5, bf16[8192,256]{1,0:T(8,128)(2,1)} %cross_stage.14.refs_3_.refs_0_), custom_call_target="tpu_custom_call" | custom-call | flops 1073741824 | bytes 16777216 | tf_op jit(solution)/shard_map/cross_stage/pallas_call | solution.py:77
  284.3 7.5 collective-permute-done.6.partner
  291.8 58.3 %local_stages.4.refs_0_ = bf16[8192,256]{1,0:T(8,128)(2,1)} custom-call(bf16[8192,256]{1,0:T(8,128)(2,1)} %cross_stage.15.own, bf16[8192,256]{1,0:T(8,128)(2,1)} %collective-permute-done.6.partner, bf16[8,64,2,128,128]{4,3,2,1,0:T(8,128)(2,1)} %wf.5, bf16[8,64,2,128,128]{4,3,2,1,0:T(8,128)(2,1)} %refs_2_.23), custom_call_target="tpu_custom_call" | custom-call | flops 13958643712 | bytes 67108864 | tf_op jit(solution)/shard_map/local_stages/pallas_call | solution.py:191
  350.2 4.5 slice.21
  354.7 1.7 collective-permute-start
  357.6 9.3 %cross_stage.16.refs_3_.refs_0_ = bf16[8192,256]{1,0:T(8,128)(2,1)} custom-call(bf16[8192,256]{1,0:T(8,128)(2,1)} %local_stages.4.refs_0_, bf16[8192,256]{1,0:T(8,128)(2,1)} %collective-permute-done.7.refs_1_, bf16[8,64,2,128,128]{4,3,2,1,0:T(8,128)(2,1)} %refs_2_.23), custom_call_target="tpu_custom_call" | custom-call | flops 1073741824 | bytes 16777216 | tf_op jit(solution)/shard_map/cross_stage/pallas_call | solution.py:77
  366.9 80.9 %collective-permute-done.refs_1_ = bf16[8192,256]{1,0:T(8,128)(2,1)} collective-permute-done((bf16[8192,256]{1,0:T(8,128)(2,1)}, bf16[8192,256]{1,0:T(8,128)(2,1)}, u32[]{:S(2)}, u32[]{:S(2)}) %collective-permute-start) | collective-permute-done | bytes 4194336 | tf_op jit(solution)/shard_map/ppermute | solution.py:213
  447.9 9.3 %cross_stage.17.own = bf16[8192,256]{1,0:T(8,128)(2,1)} custom-call(bf16[8192,768]{1,0:T(8,128)(2,1)} %refs_0_.7, bf16[8192,256]{1,0:T(8,128)(2,1)} %collective-permute-done.refs_1_, bf16[8,64,2,128,128]{4,3,2,1,0:T(8,128)(2,1)} %wf.5, bf16[8192,256]{1,0:T(8,128)(2,1)} %cross_stage.16.refs_3_.refs_0_), custom_call_target="tpu_custom_call" | custom-call | flops 1073741824 | bytes 16777216 | tf_op jit(solution)/shard_map/cross_stage/pallas_call | solution.py:77
  457.2 7.5 collective-permute-done.8.partner
  464.7 58.3 %local_stages.5.refs_0_ = bf16[8192,256]{1,0:T(8,128)(2,1)} custom-call(bf16[8192,256]{1,0:T(8,128)(2,1)} %cross_stage.17.own, bf16[8192,256]{1,0:T(8,128)(2,1)} %collective-permute-done.8.partner, bf16[8,64,2,128,128]{4,3,2,1,0:T(8,128)(2,1)} %wf.5, bf16[8,64,2,128,128]{4,3,2,1,0:T(8,128)(2,1)} %refs_2_.23), custom_call_target="tpu_custom_call" | custom-call | flops 13958643712 | bytes 67108864 | tf_op jit(solution)/shard_map/local_stages/pallas_call | solution.py:191
  525.2 5.4 collective-permute-done.9.refs_1_
  530.5 11.1 %cross_stage.20.refs_0_ = bf16[6656,256]{1,0:T(8,128)(2,1)} custom-call(bf16[8192,256]{1,0:T(8,128)(2,1)} %local_stages.5.refs_0_, bf16[8192,256]{1,0:T(8,128)(2,1)} %collective-permute-done.9.refs_1_, bf16[8,64,2,128,128]{4,3,2,1,0:T(8,128)(2,1)} %refs_2_.23), custom_call_target="tpu_custom_call" | custom-call | flops 872415232 | bytes 13631488 | tf_op jit(solution)/shard_map/cross_stage/pallas_call | solution.py:77
  544.5 2.3 cross_stage.19.own
  548.1 2.1 cross_stage.18.refs_3_.refs_4_.own
  551.9 65.0 %collective-permute-done.14.refs_1_ = bf16[8192,256]{1,0:T(8,128)(2,1)} collective-permute-done((bf16[8192,256]{1,0:T(8,128)(2,1)}, bf16[8192,256]{1,0:T(8,128)(2,1)}, u32[]{:S(2)}, u32[]{:S(2)}) %collective-permute-start.14) | collective-permute-done | bytes 4194336 | tf_op jit(solution)/shard_map/ppermute | solution.py:213
  616.9 9.3 %cross_stage.21.refs_3_ = bf16[8192,768]{1,0:T(8,128)(2,1)} custom-call(bf16[8192,256]{1,0:T(8,128)(2,1)} %cross_stage.14.refs_3_.refs_0_, bf16[8192,256]{1,0:T(8,128)(2,1)} %collective-permute-done.14.refs_1_, bf16[8,64,2,128,128]{4,3,2,1,0:T(8,128)(2,1)} %refs_2_.23, bf16[512,256]{1,0:T(8,128)(2,1)} %cross_stage.18.refs_3_.refs_4_.own), custom_call_target="tpu_custom_call" | custom-call | flops 1073741824 | bytes 16777216 | tf_op jit(solution)/shard_map/cross_stage/pallas_call | solution.py:77
  626.2 80.6 %collective-permute-done.13.refs_1_ = bf16[8192,256]{1,0:T(8,128)(2,1)} collective-permute-done((bf16[8192,256]{1,0:T(8,128)(2,1)}, bf16[8192,256]{1,0:T(8,128)(2,1)}, u32[]{:S(2)}, u32[]{:S(2)}) %collective-permute-start.13) | collective-permute-done | bytes 4194336 | tf_op jit(solution)/shard_map/ppermute | solution.py:213
  706.8 9.3 %cross_stage.22.refs_3_ = bf16[8192,768]{1,0:T(8,128)(2,1)} custom-call(bf16[8192,256]{1,0:T(8,128)(2,1)} %cross_stage.16.refs_3_.refs_0_, bf16[8192,256]{1,0:T(8,128)(2,1)} %collective-permute-done.13.refs_1_, bf16[8,64,2,128,128]{4,3,2,1,0:T(8,128)(2,1)} %refs_2_.23, bf16[8192,768]{1,0:T(8,128)(2,1)} %cross_stage.21.refs_3_, ...), custom_call_target="tpu_custom_call", output_to_operand_aliasing={{}: (3, {})} | custom-call | flops 1073741824 | bytes 16777216 | tf_op jit(solution)/shard_map/cross_stage/pallas_call | solution.py:77
  716.1 63.7 %collective-permute-done.12.refs_1_ = bf16[6656,256]{1,0:T(8,128)(2,1)} collective-permute-done((bf16[6656,256]{1,0:T(8,128)(2,1)}, bf16[6656,256]{1,0:T(8,128)(2,1)}, u32[]{:S(2)}, u32[]{:S(2)}) %collective-permute-start.12) | collective-permute-done | bytes 3407904 | tf_op jit(solution)/shard_map/ppermute | solution.py:213
  779.8 11.1 %cross_stage.23.into = bf16[8192,768]{1,0:T(8,128)(2,1)} custom-call(bf16[6656,256]{1,0:T(8,128)(2,1)} %cross_stage.20.refs_0_, bf16[6656,256]{1,0:T(8,128)(2,1)} %collective-permute-done.12.refs_1_, bf16[8,64,2,128,128]{4,3,2,1,0:T(8,128)(2,1)} %refs_2_.23, bf16[8192,768]{1,0:T(8,128)(2,1)} %cross_stage.22.refs_3_, ...), custom_call_target="tpu_custom_call", output_to_operand_aliasing={{}: (3, {})} | custom-call | flops 872415232 | bytes 13631488 | tf_op jit(solution)/shard_map/cross_stage/pallas_call | solution.py:77
  792.1 4.0 collective-permute-done.10.partner
  (27 shorter events, 14.4 us)
Async XLA Ops:
  5.1 97.3 %collective-permute-start.2 = (bf16[7168,256]{1,0:T(8,128)(2,1)}, bf16[7168,256]{1,0:T(8,128)(2,1)}, u32[]{:S(2)}, u32[]{:S(2)}) collective-permute-start(bf16[7168,256]{1,0:T(8,128)(2,1)} %slice.19), channel_id=1, source_target_pairs={{0,2},{1,3},{2,0},{3,1},{4,6},{5,7},{6,4},{7,5}} | collective-permute-start | bytes 11010056 | tf_op jit(solution)/shard_map/ppermute | solution.py:213
  8.5 90.8 %collective-permute-start.3 = (bf16[1024,256]{1,0:T(8,128)(2,1)S(1)}, bf16[1024,256]{1,0:T(8,128)(2,1)S(1)}, u32[]{:S(2)}, u32[]{:S(2)}) collective-permute-start(bf16[1024,256]{1,0:T(8,128)(2,1)S(1)} %slice.18), channel_id=1, source_target_pairs={{0,2},{1,3},{2,0},{3,1},{4,6},{5,7},{6,4},{7,5}} | collective-permute-start | bytes 1572872 | tf_op jit(solution)/shard_map/ppermute | solution.py:213
  99.2 0.8 copy-start.2
  111.3 7.5 collective-permute-start.4
  177.2 7.5 collective-permute-start.5
  181.8 93.2 %collective-permute-start.1 = (bf16[8192,256]{1,0:T(8,128)(2,1)}, bf16[8192,256]{1,0:T(8,128)(2,1)}, u32[]{:S(2)}, u32[]{:S(2)}) collective-permute-start(bf16[8192,256]{1,0:T(8,128)(2,1)} %slice.20), channel_id=1, source_target_pairs={{0,2},{1,3},{2,0},{3,1},{4,6},{5,7},{6,4},{7,5}} | collective-permute-start | bytes 12582920 | tf_op jit(solution)/shard_map/ppermute | solution.py:213
  284.3 7.5 collective-permute-start.6
  350.1 7.5 collective-permute-start.7
  354.7 93.2 %collective-permute-start = (bf16[8192,256]{1,0:T(8,128)(2,1)}, bf16[8192,256]{1,0:T(8,128)(2,1)}, u32[]{:S(2)}, u32[]{:S(2)}) collective-permute-start(bf16[8192,256]{1,0:T(8,128)(2,1)} %slice.21), channel_id=1, source_target_pairs={{0,2},{1,3},{2,0},{3,1},{4,6},{5,7},{6,4},{7,5}} | collective-permute-start | bytes 12582920 | tf_op jit(solution)/shard_map/ppermute | solution.py:213
  457.2 7.5 collective-permute-start.8
  523.0 7.5 collective-permute-start.9
  523.2 93.8 %collective-permute-start.14 = (bf16[8192,256]{1,0:T(8,128)(2,1)}, bf16[8192,256]{1,0:T(8,128)(2,1)}, u32[]{:S(2)}, u32[]{:S(2)}) collective-permute-start(bf16[8192,256]{1,0:T(8,128)(2,1)} %cross_stage.14.refs_3_.refs_0_), channel_id=1, source_target_pairs={{0,2},{1,3},{2,0},{3,1},{4,6},{5,7},{6,4},{7,5}} | collective-permute-start | bytes 12582920 | tf_op jit(solution)/shard_map/ppermute | solution.py:213
  524.9 181.9 %collective-permute-start.13 = (bf16[8192,256]{1,0:T(8,128)(2,1)}, bf16[8192,256]{1,0:T(8,128)(2,1)}, u32[]{:S(2)}, u32[]{:S(2)}) collective-permute-start(bf16[8192,256]{1,0:T(8,128)(2,1)} %cross_stage.16.refs_3_.refs_0_), channel_id=1, source_target_pairs={{0,2},{1,3},{2,0},{3,1},{4,6},{5,7},{6,4},{7,5}} | collective-permute-start | bytes 12582920 | tf_op jit(solution)/shard_map/ppermute | solution.py:213
  541.7 238.2 %collective-permute-start.12 = (bf16[6656,256]{1,0:T(8,128)(2,1)}, bf16[6656,256]{1,0:T(8,128)(2,1)}, u32[]{:S(2)}, u32[]{:S(2)}) collective-permute-start(bf16[6656,256]{1,0:T(8,128)(2,1)} %cross_stage.20.refs_0_), channel_id=1, source_target_pairs={{0,2},{1,3},{2,0},{3,1},{4,6},{5,7},{6,4},{7,5}} | collective-permute-start | bytes 10223624 | tf_op jit(solution)/shard_map/ppermute | solution.py:213
  546.8 244.1 %collective-permute-start.11 = (bf16[1024,256]{1,0:T(8,128)(2,1)}, bf16[1024,256]{1,0:T(8,128)(2,1)S(1)}, u32[]{:S(2)}, u32[]{:S(2)}) collective-permute-start(bf16[1024,256]{1,0:T(8,128)(2,1)} %cross_stage.19.own), channel_id=1, source_target_pairs={{0,2},{1,3},{2,0},{3,1},{4,6},{5,7},{6,4},{7,5}} | collective-permute-start | bytes 1572872 | tf_op jit(solution)/shard_map/ppermute | solution.py:213
  550.2 245.9 %collective-permute-start.10 = (bf16[512,256]{1,0:T(8,128)(2,1)}, bf16[512,256]{1,0:T(8,128)(2,1)S(1)}, u32[]{:S(2)}, u32[]{:S(2)}) collective-permute-start(bf16[512,256]{1,0:T(8,128)(2,1)} %cross_stage.18.refs_3_.refs_4_.own), channel_id=1, source_target_pairs={{0,2},{1,3},{2,0},{3,1},{4,6},{5,7},{6,4},{7,5}} | collective-permute-start | bytes 786440 | tf_op jit(solution)/shard_map/ppermute | solution.py:213
  716.1 74.9 %copy-start.1 = (bf16[1024,256]{1,0:T(8,128)(2,1)S(1)}, bf16[1024,256]{1,0:T(8,128)(2,1)}, u32[]{:S(2)}) copy-start(bf16[1024,256]{1,0:T(8,128)(2,1)} %cross_stage.19.own) | copy-start | bytes 1572868
  791.0 5.0 copy-start

commit v2 on v0

--- a/solution.py
+++ b/solution.py
@@ -11,7 +11,7 @@
 
 WIDTH = 256
 LAST_PIECES = (32, 16, 8, 4, 2, 2)
-FIRST_PIECES = (4, 60)
+FIRST_PIECES = (8, 56)
 TAIL_BLOCKS = 4
 
 ERFC_P = (2.326819970068386e-2, -1.387039388740657e-1, 3.687424674597105e-1, -5.824733027278666e-1, 6.210004621745983e-1,
@@ -48,13 +48,17 @@
 def cross_kernel(blocks, *refs):
     own, partner, w, out = refs[0], refs[1], refs[2], refs[-1]
     size = w.shape[-1]
-    for b in range(blocks):
-        rows = pl.ds(b * size, size)
+
+    def body(b, carry):
+        rows = pl.ds(pl.multiple_of(b * size, size), size)
         out[rows, :] = mix(w[0, b, 0], w[0, b, 1], own[rows, :], partner[rows, :]).astype(out.dtype)
+        return carry
+
+    lax.fori_loop(0, blocks, body, 0, unroll=min(blocks, 8))
 
 
 def cross_stage(own, partner, weights, stage, first, count, width, own_at, partner_at, out_shape, out_at, into=None, after=()):
-    size, blocks = weights.shape[-1], math.gcd(first, count, 8)
+    size, blocks = weights.shape[-1], math.gcd(first, count, 32)
     any_space = pl.BlockSpec(memory_space=pl.ANY)
 
     def spec(at):

time: 803 us -> 794 us (0.989)
  Pallas kernels: 275 us -> 261 us
    pallas_call x17, Pallas kernels: 97.4 us -> 83.3 us  [cross_stage(): pl.pallas_call(functools.partial(cross_kernel, blocks), grid=(count // bl...]
where the time goes in v2:
time: 794 us
  waiting for transfers between devices  497 us (63%)
  Pallas kernels  261 us (33%)
  starting transfers between devices  18.3 us (2%)
  local copies, waits for them, and re-layouts  16.9 us (2%)
    ppermute x18, waiting for transfers between devices, swap(): lax.ppermute(array, 'sp', [(device, device ^ dev_step) for device in rang...  497 us
    pallas_call x3, Pallas kernels, local_stages(): pl.pallas_call(functools.partial(local_kernel, first_steps), grid=(steps,...  175 us
    pallas_call x17, Pallas kernels, cross_stage(): pl.pallas_call(functools.partial(cross_kernel, blocks), grid=(count // bl...  83.3 us
    ppermute x18, starting transfers between devices, swap(): lax.ppermute(array, 'sp', [(device, device ^ dev_step) for device in rang...  18.3 us
  transfers between devices with their start and end apart: 18, of which 16 were waited for; matrix products, arithmetic and copies ran while one was open for 1% of the time, Pallas kernels for 8%

profile of v2, /device:TPU:0, one launch (start us, length us, event | category | flops | bytes accessed | tf_op | source)
XLA Modules:
  0.0 793.5 jit_solution(13409700218026254720)
XLA Ops:
  1.1 4.1 slice.22
  5.1 3.3 collective-permute-start.2
  8.5 90.8 %collective-permute-done.3.refs_1_ = bf16[1024,256]{1,0:T(8,128)(2,1)S(1)} collective-permute-done((bf16[1024,256]{1,0:T(8,128)(2,1)S(1)}, bf16[1024,256]{1,0:T(8,128)(2,1)S(1)}, u32[]{:S(2)}, u32[]{:S(2)}) %collective-permute-start.3) | collective-permute-done | bytes 524320 | tf_op jit(solution)/shard_map/ppermute | solution.py:217
  102.5 8.8 %cross_stage.18.own = bf16[8192,256]{1,0:T(8,128)(2,1)} custom-call(bf16[8192,768]{1,0:T(8,128)(2,1)} %refs_0_.7, bf16[7168,256]{1,0:T(8,128)(2,1)} %collective-permute-done.2.refs_1_, bf16[8,64,2,128,128]{4,3,2,1,0:T(8,128)(2,1)} %wf.5, bf16[8192,256]{1,0:T(8,128)(2,1)} %cross_stage.17.refs_3_), custom_call_target="tpu_custom_call", output_to_operand_aliasing={{}: (3, {})} | custom-call | flops 939524096 | bytes 14680064 | tf_op jit(solution)/shard_map/cross_stage/pallas_call | solution.py:81
  111.3 7.5 collective-permute-done.4.partner
  118.8 58.3 %local_stages.3.refs_0_ = bf16[8192,256]{1,0:T(8,128)(2,1)} custom-call(bf16[8192,256]{1,0:T(8,128)(2,1)} %cross_stage.18.own, bf16[8192,256]{1,0:T(8,128)(2,1)} %collective-permute-done.4.partner, bf16[8,64,2,128,128]{4,3,2,1,0:T(8,128)(2,1)} %wf.5, bf16[8,64,2,128,128]{4,3,2,1,0:T(8,128)(2,1)} %refs_2_.33), custom_call_target="tpu_custom_call" | custom-call | flops 13958643712 | bytes 67108864 | tf_op jit(solution)/shard_map/local_stages/pallas_call | solution.py:195
  177.3 4.5 slice.23
  184.6 7.2 cross_stage.19.refs_3_.refs_0_
  191.8 83.1 %collective-permute-done.1.refs_1_ = bf16[8192,256]{1,0:T(8,128)(2,1)} collective-permute-done((bf16[8192,256]{1,0:T(8,128)(2,1)}, bf16[8192,256]{1,0:T(8,128)(2,1)}, u32[]{:S(2)}, u32[]{:S(2)}) %collective-permute-start.1) | collective-permute-done | bytes 4194336 | tf_op jit(solution)/shard_map/ppermute | solution.py:217
  274.9 7.3 cross_stage.20.own
  282.2 7.5 collective-permute-done.6.partner
  289.7 58.3 %local_stages.4.refs_0_ = bf16[8192,256]{1,0:T(8,128)(2,1)} custom-call(bf16[8192,256]{1,0:T(8,128)(2,1)} %cross_stage.20.own, bf16[8192,256]{1,0:T(8,128)(2,1)} %collective-permute-done.6.partner, bf16[8,64,2,128,128]{4,3,2,1,0:T(8,128)(2,1)} %wf.5, bf16[8,64,2,128,128]{4,3,2,1,0:T(8,128)(2,1)} %refs_2_.33), custom_call_target="tpu_custom_call" | custom-call | flops 13958643712 | bytes 67108864 | tf_op jit(solution)/shard_map/local_stages/pallas_call | solution.py:195
  348.1 4.5 slice.24
  355.5 7.3 cross_stage.21.refs_3_.refs_0_
  362.8 83.0 %collective-permute-done.refs_1_ = bf16[8192,256]{1,0:T(8,128)(2,1)} collective-permute-done((bf16[8192,256]{1,0:T(8,128)(2,1)}, bf16[8192,256]{1,0:T(8,128)(2,1)}, u32[]{:S(2)}, u32[]{:S(2)}) %collective-permute-start) | collective-permute-done | bytes 4194336 | tf_op jit(solution)/shard_map/ppermute | solution.py:217
  445.8 7.3 cross_stage.22.own
  453.0 7.5 collective-permute-done.8.partner
  460.5 58.3 %local_stages.5.refs_0_ = bf16[8192,256]{1,0:T(8,128)(2,1)} custom-call(bf16[8192,256]{1,0:T(8,128)(2,1)} %cross_stage.22.own, bf16[8192,256]{1,0:T(8,128)(2,1)} %collective-permute-done.8.partner, bf16[8,64,2,128,128]{4,3,2,1,0:T(8,128)(2,1)} %wf.5, bf16[8,64,2,128,128]{4,3,2,1,0:T(8,128)(2,1)} %refs_2_.33), custom_call_target="tpu_custom_call" | custom-call | flops 13958643712 | bytes 67108864 | tf_op jit(solution)/shard_map/local_stages/pallas_call | solution.py:195
  521.0 5.3 collective-permute-done.9.refs_1_
  526.3 5.5 cross_stage.28.refs_0_
  533.6 3.4 cross_stage.27.refs_0_
  549.3 63.4 %collective-permute-done.17.refs_1_ = bf16[8192,256]{1,0:T(8,128)(2,1)} collective-permute-done((bf16[8192,256]{1,0:T(8,128)(2,1)}, bf16[8192,256]{1,0:T(8,128)(2,1)}, u32[]{:S(2)}, u32[]{:S(2)}) %collective-permute-start.17) | collective-permute-done | bytes 4194336 | tf_op jit(solution)/shard_map/ppermute | solution.py:217
  614.5 7.2 cross_stage.29.refs_3_
  621.7 80.9 %collective-permute-done.16.refs_1_ = bf16[8192,256]{1,0:T(8,128)(2,1)} collective-permute-done((bf16[8192,256]{1,0:T(8,128)(2,1)}, bf16[8192,256]{1,0:T(8,128)(2,1)}, u32[]{:S(2)}, u32[]{:S(2)}) %collective-permute-start.16) | collective-permute-done | bytes 4194336 | tf_op jit(solution)/shard_map/ppermute | solution.py:217
  704.3 43.1 %collective-permute-done.15.refs_1_ = bf16[4096,256]{1,0:T(8,128)(2,1)S(1)} collective-permute-done((bf16[4096,256]{1,0:T(8,128)(2,1)}, bf16[4096,256]{1,0:T(8,128)(2,1)S(1)}, u32[]{:S(2)}, u32[]{:S(2)}) %collective-permute-start.15) | collective-permute-done | bytes 2097184 | tf_op jit(solution)/shard_map/ppermute | solution.py:217
  749.2 7.2 cross_stage.30.refs_3_
  756.4 5.4 cross_stage.31.refs_3_
  761.8 8.2 %collective-permute-done.14.refs_1_ = bf16[2048,256]{1,0:T(8,128)(2,1)} collective-permute-done((bf16[2048,256]{1,0:T(8,128)(2,1)}, bf16[2048,256]{1,0:T(8,128)(2,1)}, u32[]{:S(2)}, u32[]{:S(2)}) %collective-permute-start.14) | collective-permute-done | bytes 1048608 | tf_op jit(solution)/shard_map/ppermute | solution.py:217
  770.0 3.4 cross_stage.32.refs_3_
  773.5 7.8 collective-permute-done.13.refs_1_
  783.7 3.1 collective-permute-done.12.partner
  787.7 4.1 collective-permute-done.11.partner
  (45 shorter events, 37.0 us)
Async XLA Ops:
  5.1 97.4 %collective-permute-start.2 = (bf16[7168,256]{1,0:T(8,128)(2,1)}, bf16[7168,256]{1,0:T(8,128)(2,1)}, u32[]{:S(2)}, u32[]{:S(2)}) collective-permute-start(bf16[7168,256]{1,0:T(8,128)(2,1)} %slice.22), channel_id=1, source_target_pairs={{0,2},{1,3},{2,0},{3,1},{4,6},{5,7},{6,4},{7,5}} | collective-permute-start | bytes 11010056 | tf_op jit(solution)/shard_map/ppermute | solution.py:217
  8.4 90.8 %collective-permute-start.3 = (bf16[1024,256]{1,0:T(8,128)(2,1)S(1)}, bf16[1024,256]{1,0:T(8,128)(2,1)S(1)}, u32[]{:S(2)}, u32[]{:S(2)}) collective-permute-start(bf16[1024,256]{1,0:T(8,128)(2,1)S(1)} %slice.21), channel_id=1, source_target_pairs={{0,2},{1,3},{2,0},{3,1},{4,6},{5,7},{6,4},{7,5}} | collective-permute-start | bytes 1572872 | tf_op jit(solution)/shard_map/ppermute | solution.py:217
  99.2 0.8 copy-start.5
  111.3 7.5 collective-permute-start.4
  177.1 7.5 collective-permute-start.5
  181.7 93.2 %collective-permute-start.1 = (bf16[8192,256]{1,0:T(8,128)(2,1)}, bf16[8192,256]{1,0:T(8,128)(2,1)}, u32[]{:S(2)}, u32[]{:S(2)}) collective-permute-start(bf16[8192,256]{1,0:T(8,128)(2,1)} %slice.23), channel_id=1, source_target_pairs={{0,2},{1,3},{2,0},{3,1},{4,6},{5,7},{6,4},{7,5}} | collective-permute-start | bytes 12582920 | tf_op jit(solution)/shard_map/ppermute | solution.py:217
  282.2 7.5 collective-permute-start.6
  348.0 7.5 collective-permute-start.7
  352.6 93.2 %collective-permute-start = (bf16[8192,256]{1,0:T(8,128)(2,1)}, bf16[8192,256]{1,0:T(8,128)(2,1)}, u32[]{:S(2)}, u32[]{:S(2)}) collective-permute-start(bf16[8192,256]{1,0:T(8,128)(2,1)} %slice.24), channel_id=1, source_target_pairs={{0,2},{1,3},{2,0},{3,1},{4,6},{5,7},{6,4},{7,5}} | collective-permute-start | bytes 12582920 | tf_op jit(solution)/shard_map/ppermute | solution.py:217
  453.0 7.5 collective-permute-start.8
  518.8 7.5 collective-permute-start.9
  519.0 93.8 %collective-permute-start.17 = (bf16[8192,256]{1,0:T(8,128)(2,1)}, bf16[8192,256]{1,0:T(8,128)(2,1)}, u32[]{:S(2)}, u32[]{:S(2)}) collective-permute-start(bf16[8192,256]{1,0:T(8,128)(2,1)} %cross_stage.19.refs_3_.refs_0_), channel_id=1, source_target_pairs={{0,2},{1,3},{2,0},{3,1},{4,6},{5,7},{6,4},{7,5}} | collective-permute-start | bytes 12582920 | tf_op jit(solution)/shard_map/ppermute | solution.py:217
  520.7 181.9 %collective-permute-start.16 = (bf16[8192,256]{1,0:T(8,128)(2,1)}, bf16[8192,256]{1,0:T(8,128)(2,1)}, u32[]{:S(2)}, u32[]{:S(2)}) collective-permute-start(bf16[8192,256]{1,0:T(8,128)(2,1)} %cross_stage.21.refs_3_.refs_0_), channel_id=1, source_target_pairs={{0,2},{1,3},{2,0},{3,1},{4,6},{5,7},{6,4},{7,5}} | collective-permute-start | bytes 12582920 | tf_op jit(solution)/shard_map/ppermute | solution.py:217
  531.8 215.6 %collective-permute-start.15 = (bf16[4096,256]{1,0:T(8,128)(2,1)}, bf16[4096,256]{1,0:T(8,128)(2,1)S(1)}, u32[]{:S(2)}, u32[]{:S(2)}) collective-permute-start(bf16[4096,256]{1,0:T(8,128)(2,1)} %cross_stage.28.refs_0_), channel_id=1, source_target_pairs={{0,2},{1,3},{2,0},{3,1},{4,6},{5,7},{6,4},{7,5}} | collective-permute-start | bytes 6291464 | tf_op jit(solution)/shard_map/ppermute | solution.py:217
  537.0 233.0 %collective-permute-start.14 = (bf16[2048,256]{1,0:T(8,128)(2,1)}, bf16[2048,256]{1,0:T(8,128)(2,1)}, u32[]{:S(2)}, u32[]{:S(2)}) collective-permute-start(bf16[2048,256]{1,0:T(8,128)(2,1)} %cross_stage.27.refs_0_), channel_id=1, source_target_pairs={{0,2},{1,3},{2,0},{3,1},{4,6},{5,7},{6,4},{7,5}} | collective-permute-start | bytes 3145736 | tf_op jit(solution)/shard_map/ppermute | solution.py:217
  539.8 241.4 %collective-permute-start.13 = (bf16[1024,256]{1,0:T(8,128)(2,1)}, bf16[1024,256]{1,0:T(8,128)(2,1)}, u32[]{:S(2)}, u32[]{:S(2)}) collective-permute-start(bf16[1024,256]{1,0:T(8,128)(2,1)} %cross_stage.26.refs_0_), channel_id=1, source_target_pairs={{0,2},{1,3},{2,0},{3,1},{4,6},{5,7},{6,4},{7,5}} | collective-permute-start | bytes 1572872 | tf_op jit(solution)/shard_map/ppermute | solution.py:217
  549.3 153.3 %copy-start = (bf16[256,256]{1,0:T(8,128)(2,1)S(1)}, bf16[256,256]{1,0:T(8,128)(2,1)}, u32[]{:S(2)}) copy-start(bf16[256,256]{1,0:T(8,128)(2,1)} %cross_stage.23.refs_3_.refs_4_.own) | copy-start | bytes 393220
  549.3 198.1 %copy-start.3 = (bf16[256,256]{1,0:T(8,128)(2,1)S(1)}, bf16[256,256]{1,0:T(8,128)(2,1)}, u32[]{:S(2)}) copy-start(bf16[256,256]{1,0:T(8,128)(2,1)} %cross_stage.24.own) | copy-start | bytes 393220
  612.7 174.0 %collective-permute-start.12 = (bf16[512,256]{1,0:T(8,128)(2,1)}, bf16[512,256]{1,0:T(8,128)(2,1)S(1)}, u32[]{:S(2)}, u32[]{:S(2)}) collective-permute-start(bf16[512,256]{1,0:T(8,128)(2,1)} %cross_stage.25.own), channel_id=1, source_target_pairs={{0,2},{1,3},{2,0},{3,1},{4,6},{5,7},{6,4},{7,5}} | collective-permute-start | bytes 786440 | tf_op jit(solution)/shard_map/ppermute | solution.py:217
  702.6 90.0 %collective-permute-start.10 = (bf16[256,256]{1,0:T(8,128)(2,1)S(1)}, bf16[256,256]{1,0:T(8,128)(2,1)S(1)}, u32[]{:S(2)}, u32[]{:S(2)}) collective-permute-start(bf16[256,256]{1,0:T(8,128)(2,1)S(1)} %copy-done), channel_id=1, source_target_pairs={{0,2},{1,3},{2,0},{3,1},{4,6},{5,7},{6,4},{7,5}} | collective-permute-start | bytes 393224 | tf_op jit(solution)/shard_map/ppermute | solution.py:217
  747.4 9.0 %copy-start.4 = (bf16[4096,256]{1,0:T(8,128)(2,1)}, bf16[4096,256]{1,0:T(8,128)(2,1)S(1)}, u32[]{:S(2)}) copy-start(bf16[4096,256]{1,0:T(8,128)(2,1)S(1)} %collective-permute-done.15.refs_1_) | copy-start | bytes 6291460
  747.4 44.3 %collective-permute-start.11 = (bf16[256,256]{1,0:T(8,128)(2,1)S(1)}, bf16[256,256]{1,0:T(8,128)(2,1)S(1)}, u32[]{:S(2)}, u32[]{:S(2)}) collective-permute-start(bf16[256,256]{1,0:T(8,128)(2,1)S(1)} %copy-done.3), channel_id=1, source_target_pairs={{0,2},{1,3},{2,0},{3,1},{4,6},{5,7},{6,4},{7,5}} | collective-permute-start | bytes 393224 | tf_op jit(solution)/shard_map/ppermute | solution.py:217
  773.5 13.3 %copy-start.2 = (bf16[512,256]{1,0:T(8,128)(2,1)S(1)}, bf16[512,256]{1,0:T(8,128)(2,1)}, u32[]{:S(2)}) copy-start(bf16[512,256]{1,0:T(8,128)(2,1)} %cross_stage.25.own) | copy-start | bytes 786436
  791.8 0.9 copy-start.1

commit v3 on v2

--- a/solution.py
+++ b/solution.py
@@ -43,6 +43,34 @@
     weights = jnp.concatenate([w_own, w_cross], axis=1)
     blocks = jnp.concatenate([z_own, z_cross], axis=0)
     return jnp.dot(weights, blocks, preferred_element_type=jnp.float32)
+
+
+def take_kernel(row, rows, col, parts, source, out, held, sem_in, sem_out):
+    width, step = out.shape[1], rows // parts
+    ins = [pltpu.make_async_copy(source.at[pl.ds(row + p * step, step), pl.ds(col, width)], held.at[pl.ds(p * step, step), :], sem_in.at[p])
+           for p in range(parts)]
+    outs = [pltpu.make_async_copy(held.at[pl.ds(p * step, step), :], out.at[pl.ds(p * step, step), :], sem_out.at[p])
+            for p in range(parts)]
+    for copy in ins:
+        copy.start()
+    for p in range(parts):
+        ins[p].wait()
+        outs[p].start()
+    for copy in outs:
+        copy.wait()
+
+
+def take(source, row, rows, col, width, parts):
+    any_space = pl.BlockSpec(memory_space=pl.ANY)
+    return pl.pallas_call(
+        functools.partial(take_kernel, row, rows, col, parts),
+        out_shape=jax.ShapeDtypeStruct((rows, width), source.dtype),
+        in_specs=[any_space],
+        out_specs=any_space,
+        scratch_shapes=[pltpu.VMEM((rows, width), source.dtype), pltpu.SemaphoreType.DMA((parts,)), pltpu.SemaphoreType.DMA((parts,))],
+        cost_estimate=pl.CostEstimate(flops=rows * width, bytes_accessed=4 * rows * width, transcendentals=0),
+        name="take",
+    )(source)
 
 
 def cross_kernel(blocks, *refs):
@@ -95,15 +123,12 @@
 def tail_kernel(count, first, col, own, partner, w, into, out, mixed, sem):
     del into
     size, width = w.shape[-1], own.shape[1]
-    copies = []
     for b in range(count):
         rows = pl.ds(b * size, size)
         mixed[rows, :] = mix(w[b, 0], w[b, 1], own[rows, :], partner[rows, :]).astype(mixed.dtype)
-        target = out.at[pl.ds((first + b) * size, size), pl.ds(col * width, width)]
-        copies.append(pltpu.make_async_copy(mixed.at[rows, :], target, sem.at[b]))
-        copies[-1].start()
-    for copy in copies:
-        copy.wait()
+    copy = pltpu.make_async_copy(mixed, out.at[pl.ds(first * size, count * size), pl.ds(col * width, width)], sem)
+    copy.start()
+    copy.wait()
 
 
 def tail_stage(own, partner, weights, first, count, col, into):
@@ -114,7 +139,7 @@
         out_shape=jax.ShapeDtypeStruct(into.shape, into.dtype),
         in_specs=[vmem, vmem, vmem, any_space],
         out_specs=any_space,
-        scratch_shapes=[pltpu.VMEM((count * size, width), own.dtype), pltpu.SemaphoreType.DMA((count,))],
+        scratch_shapes=[pltpu.VMEM((count * size, width), own.dtype), pltpu.SemaphoreType.DMA],
         input_output_aliases={3: 0},
         compiler_params=pltpu.CompilerParams(vmem_limit_bytes=4 * 1024 * 1024),
         cost_estimate=pl.CostEstimate(
@@ -223,13 +248,15 @@
         far = (2 ** (stages - 1)) // local
         near = far // 2
         width = WIDTH
-        sent, source = [], signal
+        sent = []
         for c in range(cols // width):
             pieces = FIRST_PIECES if c == 0 else (local,)
             first, parts = 0, []
-            for count in pieces:
-                piece = source[first * size:(first + count) * size, c * width:(c + 1) * width]
-                source, piece = lax.optimization_barrier((source, piece))
+            for k, count in enumerate(pieces):
+                if c == k == 0:
+                    piece = signal[:count * size, :width]
+                else:
+                    piece = take(signal, first * size, count * size, c * width, width, 2)
                 parts.append((first, count, swap(piece, far)))
                 first += count
             sent.append(parts)

time: 794 us -> 791 us (level)
  local copies, waits for them, and re-layouts: 16.9 us -> 3.87 us
  Pallas kernels: 261 us -> 272 us
    slice x4 -> x1, local copies, waits for them, and re-layouts: 14.1 us -> 1.08 us  [device_program(): piece = signal[:count * size, :width]]
    pallas_call x0 -> x3, Pallas kernels: none -> 10.6 us  [take(): pl.pallas_call(functools.partial(take_kernel, row, rows, col, parts), out...]
  transfers between devices with their start and end apart: 18 -> 18, of which waited for: 16 -> 16; matrix products, arithmetic and copies ran while one was open for 1% -> 0% of each run, Pallas kernels for 8% -> 9%
where the time goes in v3:
time: 791 us; the launch traced here: 790 us
  waiting for transfers between devices  496 us (63%)
  Pallas kernels  272 us (34%)
  starting transfers between devices  18.3 us (2%)
    ppermute x18, waiting for transfers between devices, swap(): lax.ppermute(array, 'sp', [(device, device ^ dev_step) for device in rang...  496 us
    pallas_call x3, Pallas kernels, local_stages(): pl.pallas_call(functools.partial(local_kernel, first_steps), grid=(steps,...  175 us
    pallas_call x17, Pallas kernels, cross_stage(): pl.pallas_call(functools.partial(cross_kernel, blocks), grid=(count // bl...  83.3 us
    ppermute x18, starting transfers between devices, swap(): lax.ppermute(array, 'sp', [(device, device ^ dev_step) for device in rang...  18.3 us
  transfers between devices with their start and end apart: 18, of which 16 were waited for; matrix products, arithmetic and copies ran while one was open for 0% of the time, Pallas kernels for 9%

profile of v3, /device:TPU:0, one launch (start us, length us, event | category | flops | bytes accessed | tf_op | source)
XLA Modules:
  0.0 790.1 jit_solution(3954043761873317060)
XLA Ops:
  0.0 3.3 take.5
  3.3 3.3 collective-permute-start.2
  7.8 89.7 %collective-permute-done.3.refs_1_ = bf16[1024,256]{1,0:T(8,128)(2,1)S(1)} collective-permute-done((bf16[1024,256]{1,0:T(8,128)(2,1)S(1)}, bf16[1024,256]{1,0:T(8,128)(2,1)S(1)}, u32[]{:S(2)}, u32[]{:S(2)}) %collective-permute-start.3) | collective-permute-done | bytes 524320 | tf_op jit(solution)/shard_map/ppermute | solution.py:242
  100.7 8.8 %cross_stage.18.own = bf16[8192,256]{1,0:T(8,128)(2,1)} custom-call(bf16[8192,768]{1,0:T(8,128)(2,1)} %refs_0_.7, bf16[7168,256]{1,0:T(8,128)(2,1)} %collective-permute-done.2.refs_1_, bf16[8,64,2,128,128]{4,3,2,1,0:T(8,128)(2,1)} %wf.5, bf16[8192,256]{1,0:T(8,128)(2,1)} %cross_stage.17.refs_3_), custom_call_target="tpu_custom_call", output_to_operand_aliasing={{}: (3, {})} | custom-call | flops 939524096 | bytes 14680064 | tf_op jit(solution)/shard_map/cross_stage/pallas_call | solution.py:109
  109.5 7.5 collective-permute-done.4.partner
  117.0 58.3 %local_stages.3.refs_0_ = bf16[8192,256]{1,0:T(8,128)(2,1)} custom-call(bf16[8192,256]{1,0:T(8,128)(2,1)} %cross_stage.18.own, bf16[8192,256]{1,0:T(8,128)(2,1)} %collective-permute-done.4.partner, bf16[8,64,2,128,128]{4,3,2,1,0:T(8,128)(2,1)} %wf.5, bf16[8,64,2,128,128]{4,3,2,1,0:T(8,128)(2,1)} %refs_2_.33), custom_call_target="tpu_custom_call" | custom-call | flops 13958643712 | bytes 67108864 | tf_op jit(solution)/shard_map/local_stages/pallas_call | solution.py:220
  175.5 3.6 take.4
  182.8 7.2 cross_stage.19.refs_3_.refs_0_
  190.1 82.3 %collective-permute-done.1.refs_1_ = bf16[8192,256]{1,0:T(8,128)(2,1)} collective-permute-done((bf16[8192,256]{1,0:T(8,128)(2,1)}, bf16[8192,256]{1,0:T(8,128)(2,1)}, u32[]{:S(2)}, u32[]{:S(2)}) %collective-permute-start.1) | collective-permute-done | bytes 4194336 | tf_op jit(solution)/shard_map/ppermute | solution.py:242
  272.3 7.3 cross_stage.20.own
  279.6 7.5 collective-permute-done.6.partner
  287.1 58.3 %local_stages.4.refs_0_ = bf16[8192,256]{1,0:T(8,128)(2,1)} custom-call(bf16[8192,256]{1,0:T(8,128)(2,1)} %cross_stage.20.own, bf16[8192,256]{1,0:T(8,128)(2,1)} %collective-permute-done.6.partner, bf16[8,64,2,128,128]{4,3,2,1,0:T(8,128)(2,1)} %wf.5, bf16[8,64,2,128,128]{4,3,2,1,0:T(8,128)(2,1)} %refs_2_.33), custom_call_target="tpu_custom_call" | custom-call | flops 13958643712 | bytes 67108864 | tf_op jit(solution)/shard_map/local_stages/pallas_call | solution.py:220
  345.5 3.6 take.3
  352.9 7.3 cross_stage.21.refs_3_.refs_0_
  360.2 82.2 %collective-permute-done.refs_1_ = bf16[8192,256]{1,0:T(8,128)(2,1)} collective-permute-done((bf16[8192,256]{1,0:T(8,128)(2,1)}, bf16[8192,256]{1,0:T(8,128)(2,1)}, u32[]{:S(2)}, u32[]{:S(2)}) %collective-permute-start) | collective-permute-done | bytes 4194336 | tf_op jit(solution)/shard_map/ppermute | solution.py:242
  442.4 7.3 cross_stage.22.own
  449.6 7.5 collective-permute-done.8.partner
  457.1 58.3 %local_stages.5.refs_0_ = bf16[8192,256]{1,0:T(8,128)(2,1)} custom-call(bf16[8192,256]{1,0:T(8,128)(2,1)} %cross_stage.22.own, bf16[8192,256]{1,0:T(8,128)(2,1)} %collective-permute-done.8.partner, bf16[8,64,2,128,128]{4,3,2,1,0:T(8,128)(2,1)} %wf.5, bf16[8,64,2,128,128]{4,3,2,1,0:T(8,128)(2,1)} %refs_2_.33), custom_call_target="tpu_custom_call" | custom-call | flops 13958643712 | bytes 67108864 | tf_op jit(solution)/shard_map/local_stages/pallas_call | solution.py:220
  517.6 5.3 collective-permute-done.9.refs_1_
  522.9 5.5 cross_stage.28.refs_0_
  530.1 3.5 cross_stage.27.refs_0_
  545.9 63.4 %collective-permute-done.17.refs_1_ = bf16[8192,256]{1,0:T(8,128)(2,1)} collective-permute-done((bf16[8192,256]{1,0:T(8,128)(2,1)}, bf16[8192,256]{1,0:T(8,128)(2,1)}, u32[]{:S(2)}, u32[]{:S(2)}) %collective-permute-start.17) | collective-permute-done | bytes 4194336 | tf_op jit(solution)/shard_map/ppermute | solution.py:242
  611.0 7.2 cross_stage.29.refs_3_
  618.3 80.9 %collective-permute-done.16.refs_1_ = bf16[8192,256]{1,0:T(8,128)(2,1)} collective-permute-done((bf16[8192,256]{1,0:T(8,128)(2,1)}, bf16[8192,256]{1,0:T(8,128)(2,1)}, u32[]{:S(2)}, u32[]{:S(2)}) %collective-permute-start.16) | collective-permute-done | bytes 4194336 | tf_op jit(solution)/shard_map/ppermute | solution.py:242
  700.9 43.1 %collective-permute-done.15.refs_1_ = bf16[4096,256]{1,0:T(8,128)(2,1)S(1)} collective-permute-done((bf16[4096,256]{1,0:T(8,128)(2,1)}, bf16[4096,256]{1,0:T(8,128)(2,1)S(1)}, u32[]{:S(2)}, u32[]{:S(2)}) %collective-permute-start.15) | collective-permute-done | bytes 2097184 | tf_op jit(solution)/shard_map/ppermute | solution.py:242
  745.8 7.2 cross_stage.30.refs_3_
  753.0 5.4 cross_stage.31.refs_3_
  758.4 8.2 %collective-permute-done.14.refs_1_ = bf16[2048,256]{1,0:T(8,128)(2,1)} collective-permute-done((bf16[2048,256]{1,0:T(8,128)(2,1)}, bf16[2048,256]{1,0:T(8,128)(2,1)}, u32[]{:S(2)}, u32[]{:S(2)}) %collective-permute-start.14) | collective-permute-done | bytes 1048608 | tf_op jit(solution)/shard_map/ppermute | solution.py:242
  766.6 3.4 cross_stage.32.refs_3_
  770.1 7.8 collective-permute-done.13.refs_1_
  780.3 3.0 collective-permute-done.12.partner
  784.3 4.1 collective-permute-done.11.partner
  (45 shorter events, 38.6 us)
Async XLA Ops:
  3.3 97.4 %collective-permute-start.2 = (bf16[7168,256]{1,0:T(8,128)(2,1)}, bf16[7168,256]{1,0:T(8,128)(2,1)}, u32[]{:S(2)}, u32[]{:S(2)}) collective-permute-start(bf16[7168,256]{1,0:T(8,128)(2,1)} %take.5), channel_id=1, source_target_pairs={{0,2},{1,3},{2,0},{3,1},{4,6},{5,7},{6,4},{7,5}} | collective-permute-start | bytes 11010056 | tf_op jit(solution)/shard_map/ppermute | solution.py:242
  7.7 89.7 %collective-permute-start.3 = (bf16[1024,256]{1,0:T(8,128)(2,1)S(1)}, bf16[1024,256]{1,0:T(8,128)(2,1)S(1)}, u32[]{:S(2)}, u32[]{:S(2)}) collective-permute-start(bf16[1024,256]{1,0:T(8,128)(2,1)S(1)} %slice.12), channel_id=1, source_target_pairs={{0,2},{1,3},{2,0},{3,1},{4,6},{5,7},{6,4},{7,5}} | collective-permute-start | bytes 1572872 | tf_op jit(solution)/shard_map/ppermute | solution.py:242
  97.5 0.8 copy-start.5
  109.5 7.5 collective-permute-start.4
  175.3 7.5 collective-permute-start.5
  179.1 93.2 %collective-permute-start.1 = (bf16[8192,256]{1,0:T(8,128)(2,1)}, bf16[8192,256]{1,0:T(8,128)(2,1)}, u32[]{:S(2)}, u32[]{:S(2)}) collective-permute-start(bf16[8192,256]{1,0:T(8,128)(2,1)} %take.4), channel_id=1, source_target_pairs={{0,2},{1,3},{2,0},{3,1},{4,6},{5,7},{6,4},{7,5}} | collective-permute-start | bytes 12582920 | tf_op jit(solution)/shard_map/ppermute | solution.py:242
  279.6 7.5 collective-permute-start.6
  345.4 7.5 collective-permute-start.7
  349.2 93.2 %collective-permute-start = (bf16[8192,256]{1,0:T(8,128)(2,1)}, bf16[8192,256]{1,0:T(8,128)(2,1)}, u32[]{:S(2)}, u32[]{:S(2)}) collective-permute-start(bf16[8192,256]{1,0:T(8,128)(2,1)} %take.3), channel_id=1, source_target_pairs={{0,2},{1,3},{2,0},{3,1},{4,6},{5,7},{6,4},{7,5}} | collective-permute-start | bytes 12582920 | tf_op jit(solution)/shard_map/ppermute | solution.py:242
  449.6 7.5 collective-permute-start.8
  515.4 7.5 collective-permute-start.9
  515.6 93.8 %collective-permute-start.17 = (bf16[8192,256]{1,0:T(8,128)(2,1)}, bf16[8192,256]{1,0:T(8,128)(2,1)}, u32[]{:S(2)}, u32[]{:S(2)}) collective-permute-start(bf16[8192,256]{1,0:T(8,128)(2,1)} %cross_stage.19.refs_3_.refs_0_), channel_id=1, source_target_pairs={{0,2},{1,3},{2,0},{3,1},{4,6},{5,7},{6,4},{7,5}} | collective-permute-start | bytes 12582920 | tf_op jit(solution)/shard_map/ppermute | solution.py:242
  517.3 181.9 %collective-permute-start.16 = (bf16[8192,256]{1,0:T(8,128)(2,1)}, bf16[8192,256]{1,0:T(8,128)(2,1)}, u32[]{:S(2)}, u32[]{:S(2)}) collective-permute-start(bf16[8192,256]{1,0:T(8,128)(2,1)} %cross_stage.21.refs_3_.refs_0_), channel_id=1, source_target_pairs={{0,2},{1,3},{2,0},{3,1},{4,6},{5,7},{6,4},{7,5}} | collective-permute-start | bytes 12582920 | tf_op jit(solution)/shard_map/ppermute | solution.py:242
  528.4 215.6 %collective-permute-start.15 = (bf16[4096,256]{1,0:T(8,128)(2,1)}, bf16[4096,256]{1,0:T(8,128)(2,1)S(1)}, u32[]{:S(2)}, u32[]{:S(2)}) collective-permute-start(bf16[4096,256]{1,0:T(8,128)(2,1)} %cross_stage.28.refs_0_), channel_id=1, source_target_pairs={{0,2},{1,3},{2,0},{3,1},{4,6},{5,7},{6,4},{7,5}} | collective-permute-start | bytes 6291464 | tf_op jit(solution)/shard_map/ppermute | solution.py:242
  533.6 233.0 %collective-permute-start.14 = (bf16[2048,256]{1,0:T(8,128)(2,1)}, bf16[2048,256]{1,0:T(8,128)(2,1)}, u32[]{:S(2)}, u32[]{:S(2)}) collective-permute-start(bf16[2048,256]{1,0:T(8,128)(2,1)} %cross_stage.27.refs_0_), channel_id=1, source_target_pairs={{0,2},{1,3},{2,0},{3,1},{4,6},{5,7},{6,4},{7,5}} | collective-permute-start | bytes 3145736 | tf_op jit(solution)/shard_map/ppermute | solution.py:242
  536.4 241.4 %collective-permute-start.13 = (bf16[1024,256]{1,0:T(8,128)(2,1)}, bf16[1024,256]{1,0:T(8,128)(2,1)}, u32[]{:S(2)}, u32[]{:S(2)}) collective-permute-start(bf16[1024,256]{1,0:T(8,128)(2,1)} %cross_stage.26.refs_0_), channel_id=1, source_target_pairs={{0,2},{1,3},{2,0},{3,1},{4,6},{5,7},{6,4},{7,5}} | collective-permute-start | bytes 1572872 | tf_op jit(solution)/shard_map/ppermute | solution.py:242
  545.9 153.3 %copy-start = (bf16[256,256]{1,0:T(8,128)(2,1)S(1)}, bf16[256,256]{1,0:T(8,128)(2,1)}, u32[]{:S(2)}) copy-start(bf16[256,256]{1,0:T(8,128)(2,1)} %cross_stage.23.refs_3_.refs_4_.own) | copy-start | bytes 393220
  545.9 198.1 %copy-start.3 = (bf16[256,256]{1,0:T(8,128)(2,1)S(1)}, bf16[256,256]{1,0:T(8,128)(2,1)}, u32[]{:S(2)}) copy-start(bf16[256,256]{1,0:T(8,128)(2,1)} %cross_stage.24.own) | copy-start | bytes 393220
  609.3 174.0 %collective-permute-start.12 = (bf16[512,256]{1,0:T(8,128)(2,1)}, bf16[512,256]{1,0:T(8,128)(2,1)S(1)}, u32[]{:S(2)}, u32[]{:S(2)}) collective-permute-start(bf16[512,256]{1,0:T(8,128)(2,1)} %cross_stage.25.own), channel_id=1, source_target_pairs={{0,2},{1,3},{2,0},{3,1},{4,6},{5,7},{6,4},{7,5}} | collective-permute-start | bytes 786440 | tf_op jit(solution)/shard_map/ppermute | solution.py:242
  699.2 90.1 %collective-permute-start.10 = (bf16[256,256]{1,0:T(8,128)(2,1)S(1)}, bf16[256,256]{1,0:T(8,128)(2,1)S(1)}, u32[]{:S(2)}, u32[]{:S(2)}) collective-permute-start(bf16[256,256]{1,0:T(8,128)(2,1)S(1)} %copy-done), channel_id=1, source_target_pairs={{0,2},{1,3},{2,0},{3,1},{4,6},{5,7},{6,4},{7,5}} | collective-permute-start | bytes 393224 | tf_op jit(solution)/shard_map/ppermute | solution.py:242
  744.0 9.0 %copy-start.4 = (bf16[4096,256]{1,0:T(8,128)(2,1)}, bf16[4096,256]{1,0:T(8,128)(2,1)S(1)}, u32[]{:S(2)}) copy-start(bf16[4096,256]{1,0:T(8,128)(2,1)S(1)} %collective-permute-done.15.refs_1_) | copy-start | bytes 6291460
  744.0 44.4 %collective-permute-start.11 = (bf16[256,256]{1,0:T(8,128)(2,1)S(1)}, bf16[256,256]{1,0:T(8,128)(2,1)S(1)}, u32[]{:S(2)}, u32[]{:S(2)}) collective-permute-start(bf16[256,256]{1,0:T(8,128)(2,1)S(1)} %copy-done.3), channel_id=1, source_target_pairs={{0,2},{1,3},{2,0},{3,1},{4,6},{5,7},{6,4},{7,5}} | collective-permute-start | bytes 393224 | tf_op jit(solution)/shard_map/ppermute | solution.py:242
  770.0 13.3 %copy-start.2 = (bf16[512,256]{1,0:T(8,128)(2,1)S(1)}, bf16[512,256]{1,0:T(8,128)(2,1)}, u32[]{:S(2)}) copy-start(bf16[512,256]{1,0:T(8,128)(2,1)} %cross_stage.25.own) | copy-start | bytes 786436
  788.4 0.9 copy-start.1

commit v4 on v3

--- a/solution.py
+++ b/solution.py
@@ -1,5 +1,4 @@
 import functools
-import math
 
 import jax
 import jax.numpy as jnp
@@ -11,7 +10,7 @@
 
 WIDTH = 256
 LAST_PIECES = (32, 16, 8, 4, 2, 2)
-FIRST_PIECES = (8, 56)
+FIRST_PIECES = (4, 60)
 TAIL_BLOCKS = 4
 
 ERFC_P = (2.326819970068386e-2, -1.387039388740657e-1, 3.687424674597105e-1, -5.824733027278666e-1, 6.210004621745983e-1,
@@ -86,18 +85,20 @@
 
 
 def cross_stage(own, partner, weights, stage, first, count, width, own_at, partner_at, out_shape, out_at, into=None, after=()):
-    size, blocks = weights.shape[-1], math.gcd(first, count, 32)
+    size = weights.shape[-1]
+    blocks = max(b for b in range(1, 65) if count % b == 0)
     any_space = pl.BlockSpec(memory_space=pl.ANY)
 
     def spec(at):
         row, col = at
-        return pl.BlockSpec((blocks * size, width), lambda g: (row // blocks + g, col))
+        return pl.BlockSpec((pl.Element(blocks * size), pl.Element(width)), lambda g: ((row + g * blocks) * size, col * width))
 
     operands = [own, partner, weights]
+    w_shape = tuple(map(pl.Element, (1, blocks, 2, size, size)))
     in_specs = [
         spec(own_at),
         spec(partner_at),
-        pl.BlockSpec((1, blocks, 2, size, size), lambda g: (stage, first // blocks + g, 0, 0, 0)),
+        pl.BlockSpec(w_shape, lambda g: (stage, first + g * blocks, 0, 0, 0)),
     ]
     aliases = {}
     if into is not None:

time: 791 us -> 794 us (level)
  Pallas kernels: 272 us -> 283 us
    pallas_call x17, Pallas kernels: 83.3 us -> 94.8 us  [cross_stage(): pl.pallas_call(functools.partial(cross_kernel, blocks), grid=(count // bl...]
  transfers between devices with their start and end apart: 18 -> 18, of which waited for: 16 -> 16; matrix products, arithmetic and copies ran while one was open for 0% -> 0% of each run, Pallas kernels for 9% -> 10%
where the time goes in v4:
time: 794 us
  waiting for transfers between devices  489 us (62%)
  Pallas kernels  283 us (36%)
  starting transfers between devices  18.3 us (2%)
    ppermute x18, waiting for transfers between devices, swap(): lax.ppermute(array, 'sp', [(device, device ^ dev_step) for device in rang...  489 us
    pallas_call x3, Pallas kernels, local_stages(): pl.pallas_call(functools.partial(local_kernel, first_steps), grid=(steps,...  175 us
    pallas_call x17, Pallas kernels, cross_stage(): pl.pallas_call(functools.partial(cross_kernel, blocks), grid=(count // bl...  94.8 us
    ppermute x18, starting transfers between devices, swap(): lax.ppermute(array, 'sp', [(device, device ^ dev_step) for device in rang...  18.3 us
  transfers between devices with their start and end apart: 18, of which 16 were waited for; matrix products, arithmetic and copies ran while one was open for 0% of the time, Pallas kernels for 10%

profile of v4, /device:TPU:0, one launch (start us, length us, event | category | flops | bytes accessed | tf_op | source)
XLA Modules:
  0.0 794.0 jit_solution(1213243780093243180)
XLA Ops:
  0.0 3.4 take.5
  3.5 3.3 collective-permute-start.2
  7.8 89.8 %collective-permute-done.3.refs_1_ = bf16[512,256]{1,0:T(8,128)(2,1)S(1)} collective-permute-done((bf16[512,256]{1,0:T(8,128)(2,1)S(1)}, bf16[512,256]{1,0:T(8,128)(2,1)S(1)}, u32[]{:S(2)}, u32[]{:S(2)}) %collective-permute-start.3) | collective-permute-done | bytes 262176 | tf_op jit(solution)/shard_map/ppermute | solution.py:243
  100.4 9.2 %cross_stage.18.own = bf16[8192,256]{1,0:T(8,128)(2,1)} custom-call(bf16[8192,768]{1,0:T(8,128)(2,1)} %refs_0_.7, bf16[7680,256]{1,0:T(8,128)(2,1)} %collective-permute-done.2.refs_1_, bf16[8,64,2,128,128]{4,3,2,1,0:T(8,128)(2,1)} %wf.5, bf16[8192,256]{1,0:T(8,128)(2,1)} %cross_stage.17.refs_3_), custom_call_target="tpu_custom_call", output_to_operand_aliasing={{}: (3, {})} | custom-call | flops 1006632960 | bytes 15728640 | tf_op jit(solution)/shard_map/cross_stage/pallas_call | solution.py:110
  109.6 7.5 collective-permute-done.4.partner
  117.1 58.3 %local_stages.3.refs_0_ = bf16[8192,256]{1,0:T(8,128)(2,1)} custom-call(bf16[8192,256]{1,0:T(8,128)(2,1)} %cross_stage.18.own, bf16[8192,256]{1,0:T(8,128)(2,1)} %collective-permute-done.4.partner, bf16[8,64,2,128,128]{4,3,2,1,0:T(8,128)(2,1)} %wf.5, bf16[8,64,2,128,128]{4,3,2,1,0:T(8,128)(2,1)} %refs_2_.33), custom_call_target="tpu_custom_call" | custom-call | flops 13958643712 | bytes 67108864 | tf_op jit(solution)/shard_map/local_stages/pallas_call | solution.py:221
  175.6 3.6 take.4
  182.9 9.1 %cross_stage.19.refs_3_.refs_0_ = bf16[8192,256]{1,0:T(8,128)(2,1)} custom-call(bf16[8192,256]{1,0:T(8,128)(2,1)} %local_stages.3.refs_0_, bf16[8192,256]{1,0:T(8,128)(2,1)} %collective-permute-done.5.refs_1_, bf16[8,64,2,128,128]{4,3,2,1,0:T(8,128)(2,1)} %refs_2_.33), custom_call_target="tpu_custom_call" | custom-call | flops 1073741824 | bytes 16777216 | tf_op jit(solution)/shard_map/cross_stage/pallas_call | solution.py:110
  192.0 80.4 %collective-permute-done.1.refs_1_ = bf16[8192,256]{1,0:T(8,128)(2,1)} collective-permute-done((bf16[8192,256]{1,0:T(8,128)(2,1)}, bf16[8192,256]{1,0:T(8,128)(2,1)}, u32[]{:S(2)}, u32[]{:S(2)}) %collective-permute-start.1) | collective-permute-done | bytes 4194336 | tf_op jit(solution)/shard_map/ppermute | solution.py:243
  272.4 9.2 %cross_stage.20.own = bf16[8192,256]{1,0:T(8,128)(2,1)} custom-call(bf16[8192,768]{1,0:T(8,128)(2,1)} %refs_0_.7, bf16[8192,256]{1,0:T(8,128)(2,1)} %collective-permute-done.1.refs_1_, bf16[8,64,2,128,128]{4,3,2,1,0:T(8,128)(2,1)} %wf.5, bf16[8192,256]{1,0:T(8,128)(2,1)} %cross_stage.19.refs_3_.refs_0_), custom_call_target="tpu_custom_call" | custom-call | flops 1073741824 | bytes 16777216 | tf_op jit(solution)/shard_map/cross_stage/pallas_call | solution.py:110
  281.6 7.5 collective-permute-done.6.partner
  289.1 58.3 %local_stages.4.refs_0_ = bf16[8192,256]{1,0:T(8,128)(2,1)} custom-call(bf16[8192,256]{1,0:T(8,128)(2,1)} %cross_stage.20.own, bf16[8192,256]{1,0:T(8,128)(2,1)} %collective-permute-done.6.partner, bf16[8,64,2,128,128]{4,3,2,1,0:T(8,128)(2,1)} %wf.5, bf16[8,64,2,128,128]{4,3,2,1,0:T(8,128)(2,1)} %refs_2_.33), custom_call_target="tpu_custom_call" | custom-call | flops 13958643712 | bytes 67108864 | tf_op jit(solution)/shard_map/local_stages/pallas_call | solution.py:221
  347.5 3.6 take.3
  354.9 9.1 %cross_stage.21.refs_3_.refs_0_ = bf16[8192,256]{1,0:T(8,128)(2,1)} custom-call(bf16[8192,256]{1,0:T(8,128)(2,1)} %local_stages.4.refs_0_, bf16[8192,256]{1,0:T(8,128)(2,1)} %collective-permute-done.7.refs_1_, bf16[8,64,2,128,128]{4,3,2,1,0:T(8,128)(2,1)} %refs_2_.33), custom_call_target="tpu_custom_call" | custom-call | flops 1073741824 | bytes 16777216 | tf_op jit(solution)/shard_map/cross_stage/pallas_call | solution.py:110
  364.0 80.3 %collective-permute-done.refs_1_ = bf16[8192,256]{1,0:T(8,128)(2,1)} collective-permute-done((bf16[8192,256]{1,0:T(8,128)(2,1)}, bf16[8192,256]{1,0:T(8,128)(2,1)}, u32[]{:S(2)}, u32[]{:S(2)}) %collective-permute-start) | collective-permute-done | bytes 4194336 | tf_op jit(solution)/shard_map/ppermute | solution.py:243
  444.4 9.2 %cross_stage.22.own = bf16[8192,256]{1,0:T(8,128)(2,1)} custom-call(bf16[8192,768]{1,0:T(8,128)(2,1)} %refs_0_.7, bf16[8192,256]{1,0:T(8,128)(2,1)} %collective-permute-done.refs_1_, bf16[8,64,2,128,128]{4,3,2,1,0:T(8,128)(2,1)} %wf.5, bf16[8192,256]{1,0:T(8,128)(2,1)} %cross_stage.21.refs_3_.refs_0_), custom_call_target="tpu_custom_call" | custom-call | flops 1073741824 | bytes 16777216 | tf_op jit(solution)/shard_map/cross_stage/pallas_call | solution.py:110
  453.5 7.5 collective-permute-done.8.partner
  461.0 58.3 %local_stages.5.refs_0_ = bf16[8192,256]{1,0:T(8,128)(2,1)} custom-call(bf16[8192,256]{1,0:T(8,128)(2,1)} %cross_stage.22.own, bf16[8192,256]{1,0:T(8,128)(2,1)} %collective-permute-done.8.partner, bf16[8,64,2,128,128]{4,3,2,1,0:T(8,128)(2,1)} %wf.5, bf16[8,64,2,128,128]{4,3,2,1,0:T(8,128)(2,1)} %refs_2_.33), custom_call_target="tpu_custom_call" | custom-call | flops 13958643712 | bytes 67108864 | tf_op jit(solution)/shard_map/local_stages/pallas_call | solution.py:221
  521.5 5.3 collective-permute-done.9.refs_1_
  526.8 5.5 cross_stage.28.refs_0_
  534.1 3.5 cross_stage.27.refs_0_
  549.8 63.4 %collective-permute-done.17.refs_1_ = bf16[8192,256]{1,0:T(8,128)(2,1)} collective-permute-done((bf16[8192,256]{1,0:T(8,128)(2,1)}, bf16[8192,256]{1,0:T(8,128)(2,1)}, u32[]{:S(2)}, u32[]{:S(2)}) %collective-permute-start.17) | collective-permute-done | bytes 4194336 | tf_op jit(solution)/shard_map/ppermute | solution.py:243
  615.0 9.2 %cross_stage.29.refs_3_ = bf16[8192,768]{1,0:T(8,128)(2,1)} custom-call(bf16[8192,256]{1,0:T(8,128)(2,1)} %cross_stage.19.refs_3_.refs_0_, bf16[8192,256]{1,0:T(8,128)(2,1)} %collective-permute-done.17.refs_1_, bf16[8,64,2,128,128]{4,3,2,1,0:T(8,128)(2,1)} %refs_2_.33, bf16[256,256]{1,0:T(8,128)(2,1)} %cross_stage.23.refs_3_.refs_4_.own), custom_call_target="tpu_custom_call" | custom-call | flops 1073741824 | bytes 16777216 | tf_op jit(solution)/shard_map/cross_stage/pallas_call | solution.py:110
  624.1 79.0 %collective-permute-done.16.refs_1_ = bf16[8192,256]{1,0:T(8,128)(2,1)} collective-permute-done((bf16[8192,256]{1,0:T(8,128)(2,1)}, bf16[8192,256]{1,0:T(8,128)(2,1)}, u32[]{:S(2)}, u32[]{:S(2)}) %collective-permute-start.16) | collective-permute-done | bytes 4194336 | tf_op jit(solution)/shard_map/ppermute | solution.py:243
  704.8 43.1 %collective-permute-done.15.refs_1_ = bf16[4096,256]{1,0:T(8,128)(2,1)S(1)} collective-permute-done((bf16[4096,256]{1,0:T(8,128)(2,1)}, bf16[4096,256]{1,0:T(8,128)(2,1)S(1)}, u32[]{:S(2)}, u32[]{:S(2)}) %collective-permute-start.15) | collective-permute-done | bytes 2097184 | tf_op jit(solution)/shard_map/ppermute | solution.py:243
  749.7 9.2 %cross_stage.30.refs_3_ = bf16[8192,768]{1,0:T(8,128)(2,1)} custom-call(bf16[8192,256]{1,0:T(8,128)(2,1)} %cross_stage.21.refs_3_.refs_0_, bf16[8192,256]{1,0:T(8,128)(2,1)} %collective-permute-done.16.refs_1_, bf16[8,64,2,128,128]{4,3,2,1,0:T(8,128)(2,1)} %refs_2_.33, bf16[8192,768]{1,0:T(8,128)(2,1)} %cross_stage.29.refs_3_, ...), custom_call_target="tpu_custom_call", output_to_operand_aliasing={{}: (3, {})} | custom-call | flops 1073741824 | bytes 16777216 | tf_op jit(solution)/shard_map/cross_stage/pallas_call | solution.py:110
  758.9 5.4 cross_stage.31.refs_3_
  764.3 6.2 collective-permute-done.14.refs_1_
  770.5 3.4 cross_stage.32.refs_3_
  774.0 7.8 collective-permute-done.13.refs_1_
  784.2 3.0 collective-permute-done.12.partner
  788.2 4.1 collective-permute-done.11.partner
  (45 shorter events, 38.1 us)
Async XLA Ops:
  3.5 96.9 %collective-permute-start.2 = (bf16[7680,256]{1,0:T(8,128)(2,1)}, bf16[7680,256]{1,0:T(8,128)(2,1)}, u32[]{:S(2)}, u32[]{:S(2)}) collective-permute-start(bf16[7680,256]{1,0:T(8,128)(2,1)} %take.5), channel_id=1, source_target_pairs={{0,2},{1,3},{2,0},{3,1},{4,6},{5,7},{6,4},{7,5}} | collective-permute-start | bytes 11796488 | tf_op jit(solution)/shard_map/ppermute | solution.py:243
  7.8 89.8 %collective-permute-start.3 = (bf16[512,256]{1,0:T(8,128)(2,1)S(1)}, bf16[512,256]{1,0:T(8,128)(2,1)S(1)}, u32[]{:S(2)}, u32[]{:S(2)}) collective-permute-start(bf16[512,256]{1,0:T(8,128)(2,1)S(1)} %slice.12), channel_id=1, source_target_pairs={{0,2},{1,3},{2,0},{3,1},{4,6},{5,7},{6,4},{7,5}} | collective-permute-start | bytes 786440 | tf_op jit(solution)/shard_map/ppermute | solution.py:243
  97.6 0.8 copy-start.5
  109.6 7.5 collective-permute-start.4
  175.4 7.5 collective-permute-start.5
  179.2 93.2 %collective-permute-start.1 = (bf16[8192,256]{1,0:T(8,128)(2,1)}, bf16[8192,256]{1,0:T(8,128)(2,1)}, u32[]{:S(2)}, u32[]{:S(2)}) collective-permute-start(bf16[8192,256]{1,0:T(8,128)(2,1)} %take.4), channel_id=1, source_target_pairs={{0,2},{1,3},{2,0},{3,1},{4,6},{5,7},{6,4},{7,5}} | collective-permute-start | bytes 12582920 | tf_op jit(solution)/shard_map/ppermute | solution.py:243
  281.6 7.5 collective-permute-start.6
  347.4 7.5 collective-permute-start.7
  351.2 93.2 %collective-permute-start = (bf16[8192,256]{1,0:T(8,128)(2,1)}, bf16[8192,256]{1,0:T(8,128)(2,1)}, u32[]{:S(2)}, u32[]{:S(2)}) collective-permute-start(bf16[8192,256]{1,0:T(8,128)(2,1)} %take.3), channel_id=1, source_target_pairs={{0,2},{1,3},{2,0},{3,1},{4,6},{5,7},{6,4},{7,5}} | collective-permute-start | bytes 12582920 | tf_op jit(solution)/shard_map/ppermute | solution.py:243
  453.5 7.5 collective-permute-start.8
  519.3 7.5 collective-permute-start.9
  519.5 93.8 %collective-permute-start.17 = (bf16[8192,256]{1,0:T(8,128)(2,1)}, bf16[8192,256]{1,0:T(8,128)(2,1)}, u32[]{:S(2)}, u32[]{:S(2)}) collective-permute-start(bf16[8192,256]{1,0:T(8,128)(2,1)} %cross_stage.19.refs_3_.refs_0_), channel_id=1, source_target_pairs={{0,2},{1,3},{2,0},{3,1},{4,6},{5,7},{6,4},{7,5}} | collective-permute-start | bytes 12582920 | tf_op jit(solution)/shard_map/ppermute | solution.py:243
  521.2 181.9 %collective-permute-start.16 = (bf16[8192,256]{1,0:T(8,128)(2,1)}, bf16[8192,256]{1,0:T(8,128)(2,1)}, u32[]{:S(2)}, u32[]{:S(2)}) collective-permute-start(bf16[8192,256]{1,0:T(8,128)(2,1)} %cross_stage.21.refs_3_.refs_0_), channel_id=1, source_target_pairs={{0,2},{1,3},{2,0},{3,1},{4,6},{5,7},{6,4},{7,5}} | collective-permute-start | bytes 12582920 | tf_op jit(solution)/shard_map/ppermute | solution.py:243
  532.3 215.6 %collective-permute-start.15 = (bf16[4096,256]{1,0:T(8,128)(2,1)}, bf16[4096,256]{1,0:T(8,128)(2,1)S(1)}, u32[]{:S(2)}, u32[]{:S(2)}) collective-permute-start(bf16[4096,256]{1,0:T(8,128)(2,1)} %cross_stage.28.refs_0_), channel_id=1, source_target_pairs={{0,2},{1,3},{2,0},{3,1},{4,6},{5,7},{6,4},{7,5}} | collective-permute-start | bytes 6291464 | tf_op jit(solution)/shard_map/ppermute | solution.py:243
  537.5 233.0 %collective-permute-start.14 = (bf16[2048,256]{1,0:T(8,128)(2,1)}, bf16[2048,256]{1,0:T(8,128)(2,1)}, u32[]{:S(2)}, u32[]{:S(2)}) collective-permute-start(bf16[2048,256]{1,0:T(8,128)(2,1)} %cross_stage.27.refs_0_), channel_id=1, source_target_pairs={{0,2},{1,3},{2,0},{3,1},{4,6},{5,7},{6,4},{7,5}} | collective-permute-start | bytes 3145736 | tf_op jit(solution)/shard_map/ppermute | solution.py:243
  540.3 241.5 %collective-permute-start.13 = (bf16[1024,256]{1,0:T(8,128)(2,1)}, bf16[1024,256]{1,0:T(8,128)(2,1)}, u32[]{:S(2)}, u32[]{:S(2)}) collective-permute-start(bf16[1024,256]{1,0:T(8,128)(2,1)} %cross_stage.26.refs_0_), channel_id=1, source_target_pairs={{0,2},{1,3},{2,0},{3,1},{4,6},{5,7},{6,4},{7,5}} | collective-permute-start | bytes 1572872 | tf_op jit(solution)/shard_map/ppermute | solution.py:243
  549.8 153.3 %copy-start = (bf16[256,256]{1,0:T(8,128)(2,1)S(1)}, bf16[256,256]{1,0:T(8,128)(2,1)}, u32[]{:S(2)}) copy-start(bf16[256,256]{1,0:T(8,128)(2,1)} %cross_stage.23.refs_3_.refs_4_.own) | copy-start | bytes 393220
  549.8 198.1 %copy-start.3 = (bf16[256,256]{1,0:T(8,128)(2,1)S(1)}, bf16[256,256]{1,0:T(8,128)(2,1)}, u32[]{:S(2)}) copy-start(bf16[256,256]{1,0:T(8,128)(2,1)} %cross_stage.24.own) | copy-start | bytes 393220
  613.2 174.0 %collective-permute-start.12 = (bf16[512,256]{1,0:T(8,128)(2,1)}, bf16[512,256]{1,0:T(8,128)(2,1)S(1)}, u32[]{:S(2)}, u32[]{:S(2)}) collective-permute-start(bf16[512,256]{1,0:T(8,128)(2,1)} %cross_stage.25.own), channel_id=1, source_target_pairs={{0,2},{1,3},{2,0},{3,1},{4,6},{5,7},{6,4},{7,5}} | collective-permute-start | bytes 786440 | tf_op jit(solution)/shard_map/ppermute | solution.py:243
  703.1 90.0 %collective-permute-start.10 = (bf16[256,256]{1,0:T(8,128)(2,1)S(1)}, bf16[256,256]{1,0:T(8,128)(2,1)S(1)}, u32[]{:S(2)}, u32[]{:S(2)}) collective-permute-start(bf16[256,256]{1,0:T(8,128)(2,1)S(1)} %copy-done), channel_id=1, source_target_pairs={{0,2},{1,3},{2,0},{3,1},{4,6},{5,7},{6,4},{7,5}} | collective-permute-start | bytes 393224 | tf_op jit(solution)/shard_map/ppermute | solution.py:243
  747.9 10.9 %copy-start.4 = (bf16[4096,256]{1,0:T(8,128)(2,1)}, bf16[4096,256]{1,0:T(8,128)(2,1)S(1)}, u32[]{:S(2)}) copy-start(bf16[4096,256]{1,0:T(8,128)(2,1)S(1)} %collective-permute-done.15.refs_1_) | copy-start | bytes 6291460
  748.0 44.3 %collective-permute-start.11 = (bf16[256,256]{1,0:T(8,128)(2,1)S(1)}, bf16[256,256]{1,0:T(8,128)(2,1)S(1)}, u32[]{:S(2)}, u32[]{:S(2)}) collective-permute-start(bf16[256,256]{1,0:T(8,128)(2,1)S(1)} %copy-done.3), channel_id=1, source_target_pairs={{0,2},{1,3},{2,0},{3,1},{4,6},{5,7},{6,4},{7,5}} | collective-permute-start | bytes 393224 | tf_op jit(solution)/shard_map/ppermute | solution.py:243
  774.0 13.3 %copy-start.2 = (bf16[512,256]{1,0:T(8,128)(2,1)S(1)}, bf16[512,256]{1,0:T(8,128)(2,1)}, u32[]{:S(2)}) copy-start(bf16[512,256]{1,0:T(8,128)(2,1)} %cross_stage.25.own) | copy-start | bytes 786436
  792.3 0.9 copy-start.1
